TPU v7x, 8 devices: a whole 2x2x1 slice. The times are simulated.
8 devices in a mesh: rep: 1 (over z), fsdp: 2 (over y), ep: 4 (over x, core).
Axes of the slice: x: 2, y: 2, z: 1, core: 2. Of those that a mesh axis runs over, the one named last changes fastest.
Arguments:
- tokens: bfloat16 [4096, 1024], P(('rep', 'ep', 'fsdp'))
- expert_idx: int32 [4096, 8], P(('rep', 'ep', 'fsdp'))
- gates: float32 [4096, 8], P(('rep', 'ep', 'fsdp'))
- w_gate: bfloat16 [32, 1024, 512], P('ep', 'fsdp')
- w_up: bfloat16 [32, 1024, 512], P('ep', 'fsdp')
- w_down: bfloat16 [32, 512, 1024], P('ep', None, 'fsdp')
Outputs:
- output: bfloat16 [4096, 1024], P(('rep', 'ep', 'fsdp'))
All inputs are finite; a program needn't handle non-finite values.
Results may differ from a plain program's by a relative error of at most 0.001.
Values are sent between devices in bfloat16 or wider.
A program may use at most 1 GiB of HBM per device.

v0:
```python
import jax
import jax.numpy as jnp
from jax import lax
from jax.sharding import PartitionSpec as P


def routing_matrix(expert_idx, num_experts, capacity):
    tok_count, top_k = expert_idx.shape
    flat_ids = expert_idx.reshape(tok_count * top_k)
    onehot = (flat_ids[:, None] == jnp.arange(num_experts)[None, :]).astype(jnp.int32)
    before = jnp.cumsum(onehot, axis=0) - onehot
    slot_ids = jnp.sum(before * onehot, axis=1)
    target = jnp.where(slot_ids < capacity, flat_ids * capacity + slot_ids, -1)
    select = target[:, None] == jnp.arange(num_experts * capacity)[None, :]
    return select.astype(jnp.bfloat16).reshape(tok_count, top_k, num_experts * capacity)


def solution(mesh):
    ep_size = mesh.shape['ep']
    row_spec = P(('rep', 'ep', 'fsdp'), None)

    def device_step(tokens, expert_idx, gates, w_gate, w_up, w_down):
        tok_count, top_k = expert_idx.shape
        n_local = w_gate.shape[0]
        num_experts = n_local * ep_size
        model_dim = tokens.shape[1]
        capacity = (2 * tok_count * top_k + num_experts - 1) // num_experts
        select = routing_matrix(expert_idx, num_experts, capacity)
        send_buf = jnp.einsum('tkf,td->fd', select, tokens, preferred_element_type=jnp.float32).astype(jnp.bfloat16)
        send_buf = send_buf.reshape(ep_size, n_local, capacity, model_dim)
        recv_buf = lax.all_to_all(send_buf, 'ep', 0, 0, tiled=True)
        wg_full = lax.all_gather(w_gate, 'fsdp', axis=1, tiled=True)
        wu_full = lax.all_gather(w_up, 'fsdp', axis=1, tiled=True)
        wd_full = lax.all_gather(w_down, 'fsdp', axis=2, tiled=True)
        act_a = jnp.einsum('sncd,ndf->sncf', recv_buf, wg_full, preferred_element_type=jnp.float32)
        act_b = jnp.einsum('sncd,ndf->sncf', recv_buf, wu_full, preferred_element_type=jnp.float32)
        hidden = (jax.nn.silu(act_a) * act_b).astype(jnp.bfloat16)
        expert_out = jnp.einsum('sncf,nfd->sncd', hidden, wd_full, preferred_element_type=jnp.float32).astype(jnp.bfloat16)
        back_buf = lax.all_to_all(expert_out, 'ep', 0, 0, tiled=True)
        back_rows = back_buf.reshape(num_experts * capacity, model_dim)
        pair_out = jnp.einsum('tkf,fd->tkd', select, back_rows, preferred_element_type=jnp.float32)
        mixed = tokens.astype(jnp.float32) + jnp.sum(gates[:, :, None] * pair_out, axis=1)
        return mixed.astype(jnp.bfloat16)

    return jax.shard_map(device_step, mesh=mesh, in_specs=(row_spec, row_spec, row_spec, P('ep', 'fsdp', None), P('ep', 'fsdp', None), P('ep', None, 'fsdp')), out_specs=row_spec, check_vma=False)
```

profile of v0, /device:TPU:1, one launch (start us, length us, event | category | flops | bytes accessed | tf_op | source)
XLA Modules:
  0.0 637.6 jit_solution(5273343578757345632)
XLA Ops:
  6.5 0.7 all-gather.6.cloned.1.call-update
  7.3 0.7 all-gather.4.cloned.1.call-update
  8.0 0.7 broadcast_multiply_fusion
  8.7 0.8 copy.24
  10.1 9.2 %reduce-window.6 = s32[32,32,128]{2,1,0:T(8,128)S(1)} reduce-window(s32[32,32,128]{2,1,0:T(8,128)S(1)} %fusion.27, s32[]{:T(128)} %constant.4.clone.1), window={size=1x1x128 pad=0_0x0_0x127_0}, to_apply=%region_0.0 | reduce-window | flops 16646144 | bytes 1048580 | tf_op jit(solution)/shard_map/reduce-window
  19.3 0.8 slice_reduce_fusion
  20.1 0.2 reduce-window.9
  20.3 0.2 broadcast_add_fusion
  20.5 0.4 fusion.26
  21.1 58.6 %convert_reduce_fusion = bf16[512,8192]{1,0:T(8,128)(2,1)} fusion(s32[512,8]{1,0:T(8,128)S(1)} %add_select_fusion), kind=kLoop, calls=%fused_computation | loop fusion | flops 130023424 | bytes 8404992 | tf_op jit(solution)/shard_map/tkf,td->fd/reduce_sum | solution.py:29
  79.7 15.9 %fusion.29 = bf16[8192,1024]{1,0:T(8,128)(2,1)} fusion(bf16[512,8192]{1,0:T(8,128)(2,1)} %convert_reduce_fusion, bf16[512,1024]{1,0:T(8,128)(2,1)S(1)} %copy-done), kind=kOutput, calls=%fused_computation.37 | convolution fusion | flops 8589934592 | bytes 26214400 | tf_op jit(solution)/shard_map/tkf,td->fd/dot_general | solution.py:29
  95.6 7.0 %all-to-all-start = ((bf16[4,8,256,1024]{3,2,1,0:T(8,128)(2,1)}), bf16[4,8,256,1024]{3,2,1,0:T(8,128)(2,1)}, u32[]{:S(2)}, u32[]{:S(2)}) async-start(bf16[4,8,256,1024]{3,2,1,0:T(8,128)(2,1)} %bitcast.73), calls=%async_computation | async-start | bytes 33554432 | tf_op jit(solution)/shard_map/all_to_all | solution.py:31
  102.6 0.2 all-gather.8.cloned.1.call-start
  102.9 0.5 all-gather.8.cloned.1.call-update
  103.4 9.3 %all-gather.6.cloned.1.call-done = bf16[8,1024,512]{2,1,0:T(8,128)(2,1)} async-done(((bf16[8,512,512]{2,1,0:T(8,128)(2,1)}), bf16[8,1024,512]{2,1,0:T(8,128)(2,1)}) %all-gather.6.cloned.1.call-update) | async-done | bytes 8388624 | tf_op jit(solution)/shard_map/all_gather | solution.py:33
  112.7 172.2 %all-to-all-done = bf16[4,8,256,1024]{3,2,1,0:T(8,128)(2,1)} async-done(((bf16[4,8,256,1024]{3,2,1,0:T(8,128)(2,1)}), bf16[4,8,256,1024]{3,2,1,0:T(8,128)(2,1)}, u32[]{:S(2)}, u32[]{:S(2)}) %all-to-all-start) | async-done | bytes 16777248 | tf_op jit(solution)/shard_map/all_to_all | solution.py:31
  284.9 18.0 %fusion.9 = f32[8,4,256,512]{3,2,1,0:T(8,128)} fusion(bf16[4,8,256,1024]{3,2,1,0:T(8,128)(2,1)} %all-to-all-done, bf16[8,1024,512]{2,1,0:T(8,128)(2,1)} %all-gather.6.cloned.1.call-done), kind=kOutput, calls=%fused_computation.17 | convolution fusion | flops 8589934592 | bytes 41943040 | tf_op jit(solution)/shard_map/sncd,ndf->sncf/dot_general | solution.py:36
  302.9 17.5 %all-gather.8.cloned.1.call-done = bf16[8,512,1024]{2,1,0:T(8,128)(2,1)} async-done(((bf16[8,512,512]{2,1,0:T(8,128)(2,1)}), bf16[8,512,1024]{2,1,0:T(8,128)(2,1)}) %all-gather.8.cloned.1.call-update) | async-done | bytes 8388624 | tf_op jit(solution)/shard_map/all_gather | solution.py:34
  320.3 28.1 %convert_bitcast_fusion = bf16[4,8,256,1024]{3,2,0,1:T(8,128)(2,1)} fusion(bf16[8,512,1024]{2,1,0:T(8,128)(2,1)} %all-gather.8.cloned.1.call-done, f32[8,4,256,512]{3,2,1,0:T(8,128)} %fusion.9, bf16[4,8,256,1024]{3,2,1,0:T(8,128)(2,1)} %all-to-all-done, bf16[8,1024,512]{2,1,0:T(8,128)(2,1)} %all-gather.4.cloned.1.call-done), kind=kOutput, calls=%fused_computation.15 | convolution fusion | flops 17213423616 | bytes 67108864 | tf_op jit(solution)/shard_map/sncf,nfd->sncd/dot_general | solution.py:38
  348.4 13.9 %copy.31 = bf16[4,8,256,1024]{3,2,1,0:T(8,128)(2,1)} copy(bf16[4,8,256,1024]{3,2,0,1:T(8,128)(2,1)} %convert_bitcast_fusion) | data formatting | bytes 33554432 | tf_op jit(solution)/shard_map/convert_element_type | solution.py:38
  362.3 8.0 %all-to-all-start.1 = ((bf16[4,8,256,1024]{3,2,1,0:T(8,128)(2,1)}), bf16[4,8,256,1024]{3,2,1,0:T(8,128)(2,1)}, u32[]{:S(2)}, u32[]{:S(2)}) async-start(bf16[4,8,256,1024]{3,2,1,0:T(8,128)(2,1)} %copy.31), calls=%async_computation.1 | async-start | bytes 33554432 | tf_op jit(solution)/shard_map/all_to_all | solution.py:39
  370.3 181.8 %all-to-all-done.1 = bf16[4,8,256,1024]{3,2,1,0:T(8,128)(2,1)} async-done(((bf16[4,8,256,1024]{3,2,1,0:T(8,128)(2,1)}), bf16[4,8,256,1024]{3,2,1,0:T(8,128)(2,1)}, u32[]{:S(2)}, u32[]{:S(2)}) %all-to-all-start.1) | async-done | bytes 16777248 | tf_op jit(solution)/shard_map/all_to_all | solution.py:39
  552.1 77.6 %multiply_reduce_fusion = f32[512,1024]{1,0:T(8,128)S(1)} fusion(bf16[8192,1024,1]{1,0,2:T(8,128)(2,1)} %bitcast.13, s32[512,8]{0,1:T(8,128)S(1)} %copy.28, f32[512,8]{0,1:T(8,128)S(1)} %copy-done.2), kind=kOutput, calls=%fused_computation.14 | convolution fusion | flops 68760895488 | bytes 18907136 | tf_op jit(solution)/shard_map/tkf,fd->tkd/dot_general | solution.py:41
  629.7 1.3 add_convert_fusion
  (16 shorter events, 0.8 us)
Async XLA Ops:
  6.5 73.2 %copy-start = (bf16[512,1024]{1,0:T(8,128)(2,1)S(1)}, bf16[512,1024]{1,0:T(8,128)(2,1)}, u32[]{:S(2)}) copy-start(bf16[512,1024]{1,0:T(8,128)(2,1)} %param.6) | copy-start | bytes 3145732
  6.5 106.2 %all-gather.6.cloned.1.call-start = ((), (), s32[]{:S(2)}) async-start(), calls=%async_computation.3 | async-start | bytes 12582912 | tf_op jit(solution)/shard_map/all_gather | solution.py:33
  7.3 295.6 %all-gather.4.cloned.1.call-start = ((), (), s32[]{:S(2)}) async-start(), calls=%async_computation.2 | async-start | bytes 12582912 | tf_op jit(solution)/shard_map/all_gather | solution.py:32
  95.6 189.2 %all-to-all-start = ((bf16[4,8,256,1024]{3,2,1,0:T(8,128)(2,1)}), bf16[4,8,256,1024]{3,2,1,0:T(8,128)(2,1)}, u32[]{:S(2)}, u32[]{:S(2)}) async-start(bf16[4,8,256,1024]{3,2,1,0:T(8,128)(2,1)} %bitcast.73), calls=%async_computation | async-start | bytes 33554432 | tf_op jit(solution)/shard_map/all_to_all | solution.py:31
  102.6 217.7 %all-gather.8.cloned.1.call-start = ((), (), s32[]{:S(2)}) async-start(), calls=%async_computation.4 | async-start | bytes 12582912 | tf_op jit(solution)/shard_map/all_gather | solution.py:34
  362.3 189.9 %copy-start.2 = (f32[512,8]{0,1:T(8,128)S(1)}, f32[512,8]{0,1:T(8,128)}, u32[]{:S(2)}) copy-start(f32[512,8]{0,1:T(8,128)} %param.8) | copy-start | bytes 49156
  362.3 189.9 %all-to-all-start.1 = ((bf16[4,8,256,1024]{3,2,1,0:T(8,128)(2,1)}), bf16[4,8,256,1024]{3,2,1,0:T(8,128)(2,1)}, u32[]{:S(2)}, u32[]{:S(2)}) async-start(bf16[4,8,256,1024]{3,2,1,0:T(8,128)(2,1)} %copy.31), calls=%async_computation.1 | async-start | bytes 33554432 | tf_op jit(solution)/shard_map/all_to_all | solution.py:39
  552.1 77.6 %copy-start.1 = (bf16[512,1024]{1,0:T(8,128)(2,1)S(1)}, bf16[512,1024]{1,0:T(8,128)(2,1)}, u32[]{:S(2)}) copy-start(bf16[512,1024]{1,0:T(8,128)(2,1)} %param.6) | copy-start | bytes 3145732
Sparse Core Ops, SparseCore 0:
  8.8 103.8 all-gather.5
  114.2 102.2 all-gather.3
  218.0 102.2 all-gather.7
where the time goes:
time: 639 us; the launch traced here: 638 us
  waiting for transfers between devices  383 us (60%)
  matrix products  140 us (22%)
  other arithmetic  70.8 us (11%)
  local copies, waits for them, and re-layouts  16.2 us (3%)
  starting transfers between devices  15.2 us (2%)
  between operations  13.2 us (2%)
    all_to_all x1, waiting for transfers between devices, device_step(): back_buf = lax.all_to_all(expert_out, 'ep', 0, 0, tiled=True)  182 us
    all_to_all x1, waiting for transfers between devices, device_step(): recv_buf = lax.all_to_all(send_buf, 'ep', 0, 0, tiled=True)  172 us
    dot_general x1, matrix products, device_step(): jnp.einsum('tkf,fd->tkd', select, back_rows, preferred_element_type=jnp.f...  77.6 us
    reduce_sum x1, other arithmetic, device_step(): jnp.einsum('tkf,td->fd', select, tokens, preferred_element_type=jnp.float32)  58.6 us
    dot_general x1, matrix products, device_step(): jnp.einsum('sncf,nfd->sncd', hidden, wd_full, preferred_element_type=jnp....  28.1 us
    dot_general x1, matrix products, device_step(): jnp.einsum('sncd,ndf->sncf', recv_buf, wu_full, preferred_element_type=jn...  18 us
    all_gather x1, waiting for transfers between devices, device_step(): wd_full = lax.all_gather(w_down, 'fsdp', axis=2, tiled=True)  17.5 us
    dot_general x1, matrix products, device_step(): jnp.einsum('tkf,td->fd', select, tokens, preferred_element_type=jnp.float32)  15.9 us
  transfers between devices with their start and end apart: 5, of which 4 were waited for; matrix products, arithmetic and copies ran while one was open for 17% of the time, Pallas kernels for 0%

commit v1 on v0

v1 whole, which is shorter than its diff:
```python
import functools

import jax
import jax.numpy as jnp
from jax import lax
from jax.experimental import pallas as pl
from jax.experimental.pallas import tpu as pltpu
from jax.sharding import PartitionSpec as P

MESH = pl.DeviceIdType.MESH
OWN, XN, YN, DG = 0, 1, 2, 3


def moe_kernel(num_experts, capacity, chunk, tokens_hbm, idx_ref, gates_ref, wg_hbm, wu_hbm, wd_hbm, out_ref,
               tok, w, acc, hid, gt_send, gt_recv, gcol, rx, ry,
               loc_tok_sem, tok_send, tok_recv, g_send, g_recv_sem, loc_sem, ys_sem, yr_sem,
               po_s, po_r, pf_s, pf_r, cx_s, cx_r, cy_s, cy_r):
    rows, width = out_ref.shape
    n_local = wg_hbm.shape[0]
    n_own = n_local // 2
    half_w = width // 2
    half = rows // 2
    n_chunk = half // chunk
    ep = lax.axis_index("ep")
    y = lax.axis_index("fsdp")
    c = lax.rem(ep, 2)
    x = ep // 2
    oy = 1 - y
    x_dev = {"ep": lax.rem(ep + 2, 4), "fsdp": y}
    y_dev = {"ep": ep, "fsdp": oy}
    d_dev = {"ep": lax.rem(ep + 2, 4), "fsdp": oy}
    p_dev = {"ep": ep + 1 - 2 * c, "fsdp": y}
    w_hbm = (wg_hbm, wu_hbm, wd_hbm)

    def remote(src, dst, s, r, dev):
        return pltpu.make_async_remote_copy(src_ref=src, dst_ref=dst, send_sem=s, recv_sem=r, device_id=dev, device_id_type=MESH)

    def block(b):
        return tok.at[pl.ds(b * rows, rows)]

    barrier = pltpu.get_barrier_semaphore()
    for dev in (x_dev, y_dev, d_dev, p_dev):
        pl.semaphore_signal(barrier, inc=1, device_id=dev, device_id_type=MESH)
    pl.semaphore_wait(barrier, 4)

    tok_y = remote(tokens_hbm, block(YN), tok_send.at[0], tok_recv.at[0], y_dev)
    tok_x = remote(tokens_hbm, block(XN), tok_send.at[1], tok_recv.at[1], x_dev)
    tok_d = remote(block(YN), block(DG), tok_send.at[2], tok_recv.at[2], x_dev)
    tok_l = pltpu.make_async_copy(tokens_hbm, block(OWN), loc_tok_sem)
    tok_y.start()
    tok_x.start()
    tok_l.start()

    lane = lax.broadcasted_iota(jnp.int32, (1, 128), 1)
    dest, slot = lane // n_local, lax.rem(lane, n_local)
    dx, dy = lax.rem(dest, 2), dest // 2
    ex = x + dx - 2 * x * dx
    ey = y + dy - 2 * y * dy
    sc = slot // n_own
    ec = c + sc - 2 * c * sc
    expert = (2 * ex + ec) * n_local + ey * n_own + lax.rem(slot, n_own)
    expert = jnp.where(lane < num_experts, expert, -1)
    dense = jnp.zeros((rows, 128), jnp.float32)
    chosen = jnp.zeros((rows, 128), jnp.float32)
    for j in range(idx_ref.shape[1]):
        hit = idx_ref[:, j:j + 1] == expert
        dense = jnp.where(hit, gates_ref[:, j:j + 1], dense)
        chosen = jnp.where(hit, 1.0, chosen)
    before = lax.broadcasted_iota(jnp.int32, (rows, rows), 1) < lax.broadcasted_iota(jnp.int32, (rows, rows), 0)
    taken = jnp.dot(before.astype(jnp.bfloat16), chosen.astype(jnp.bfloat16), preferred_element_type=jnp.float32)
    dense = jnp.where(taken < float(capacity), dense, 0.0)
    gt_send[...] = dense.T
    g_copies = []
    for k, (b, dev) in enumerate(((XN, x_dev), (YN, y_dev), (DG, d_dev))):
        cp = remote(gt_send.at[pl.ds(b * n_local, n_local)], gt_recv.at[k], g_send.at[k], g_recv_sem.at[k], dev)
        cp.start()
        g_copies.append(cp)
    gcol[0] = dense

    def local_w(m, i):
        return pltpu.make_async_copy(w_hbm[m].at[y * n_own + i], w.at[m, i, y], loc_sem.at[m, i])

    def send_w(m, i):
        return remote(w_hbm[m].at[oy * n_own + i], w.at[m, i, y], ys_sem.at[m, i], yr_sem.at[m, i], y_dev)

    def arrived_w(m, i):
        return remote(w_hbm[m].at[oy * n_own + i], w.at[m, i, oy], ys_sem.at[m, i], yr_sem.at[m, i], y_dev)

    def partner_own(m, i):
        return remote(w_hbm[m].at[y * n_own + i], w.at[m, n_own + i, y], po_s.at[m, i], po_r.at[m, i], p_dev)

    def partner_fwd(m, i):
        return remote(w.at[m, i, oy], w.at[m, n_own + i, oy], pf_s.at[m, i], pf_r.at[m, i], p_dev)

    for i in range(n_own):
        for m in range(3):
            send_w(m, i).start()
    for i in range(n_own):
        for m in range(3):
            local_w(m, i).start()
            partner_own(m, i).start()

    tok_y.wait_recv()
    tok_d.start()
    for k, b in enumerate((XN, YN, DG)):
        g_copies[k].wait_recv()
        padded = jnp.concatenate([gt_recv[k], jnp.zeros((128 - n_local, rows), jnp.float32)], axis=0)
        gcol[b] = padded.T

    tok_l.wait()
    tok_x.wait_recv()
    tok_d.wait_recv()

    lane2 = lax.broadcasted_iota(jnp.int32, (1, 128), 1)

    def gate_up(k, s):
        wg = w[0, s].reshape(width, w.shape[-1])
        wu = w[1, s].reshape(width, w.shape[-1])

        def step(b, carry):
            at = pl.ds(pl.multiple_of(b * rows, rows), rows)
            r = tok[at, :]
            a = jnp.dot(r, wg, preferred_element_type=jnp.float32)
            u = jnp.dot(r, wu, preferred_element_type=jnp.float32)
            hid[k, at, :] = (a * jax.nn.sigmoid(a) * u).astype(jnp.bfloat16)
            return carry

        lax.fori_loop(0, 4, step, 0)

    def weighted(k, s, b, row, n, part):
        at = pl.ds(pl.multiple_of(b * rows + row, chunk), n)
        g = jnp.sum(jnp.where(lane2 == s, gcol[b, pl.ds(pl.multiple_of(row, chunk), n), :], 0.0), axis=1, keepdims=True)
        o = jnp.dot(hid[k, at, :], w[2, s, part], preferred_element_type=jnp.float32).astype(jnp.bfloat16).astype(jnp.float32)
        return jnp.where(g != 0.0, g * o, 0.0)

    def down(k, s, first):
        def step(b, carry):
            at = pl.ds(pl.multiple_of(b * rows, rows), rows)
            for part in range(2):
                cols = pl.ds(part * half_w, half_w)
                term = weighted(k, s, b, 0, rows, part)
                acc[at, cols] = jnp.where(first, 0.0, acc[at, cols]) + term
            return carry

        lax.fori_loop(0, 4, step, 0)

    def arrive(m, i):
        arrived_w(m, i).wait_recv()
        partner_fwd(m, i).start()

    def from_partner(m, i):
        partner_own(m, i).wait_recv()
        partner_fwd(m, i).wait_recv()

    def first_half(i):
        for m in range(2):
            arrive(m, i)
            local_w(m, i).wait()
        gate_up(0, i)
        for m in range(2):
            from_partner(m, i)
        gate_up(1, n_own + i)
        arrive(2, i)
        local_w(2, i).wait()

    def round_step(i, carry):
        first_half(i)
        down(0, i, i == 0)
        from_partner(2, i)
        down(1, n_own + i, False)
        return carry

    lax.fori_loop(0, n_own - 1, round_step, 0)
    last = n_own - 1
    first_half(last)
    from_partner(2, last)

    def finish(b, row, n):
        at = pl.ds(pl.multiple_of(b * rows + row, chunk), n)
        for part in range(2):
            cols = pl.ds(part * half_w, half_w)
            acc[at, cols] = (acc[at, cols] + weighted(0, last, b, row, n, part)) + weighted(1, n_own + last, b, row, n, part)

    def part_of(b, row):
        return acc.at[pl.ds(pl.multiple_of(b * rows + row, chunk), chunk)]

    def send_x(kind, k):
        b, base = ((DG, 0), (XN, 0), (XN, half))[kind]
        return remote(part_of(b, base + k * chunk), rx.at[kind, pl.ds(pl.multiple_of(k * chunk, chunk), chunk)],
                      cx_s.at[kind, k], cx_r.at[kind, k], x_dev)

    def send_y(kind, k):
        b, base = ((DG, half), (YN, half), (YN, 0))[kind]
        return remote(part_of(b, base + k * chunk), ry.at[kind, pl.ds(pl.multiple_of(k * chunk, chunk), chunk)],
                      cy_s.at[kind, k], cy_r.at[kind, k], y_dev)

    def diag_step(k, carry):
        finish(DG, k * chunk, chunk)
        send_x(0, k).start()
        finish(DG, half + k * chunk, chunk)
        send_y(0, k).start()
        return carry

    lax.fori_loop(0, n_chunk, diag_step, 0)

    def direct_step(k, carry):
        finish(XN, k * chunk, chunk)
        send_x(1, k).start()
        finish(YN, half + k * chunk, chunk)
        send_y(1, k).start()
        return carry

    lax.fori_loop(0, n_chunk, direct_step, 0)

    def passed_step(k, carry):
        at_x = pl.ds(pl.multiple_of(XN * rows + half + k * chunk, chunk), chunk)
        at_y = pl.ds(pl.multiple_of(YN * rows + k * chunk, chunk), chunk)
        here = pl.ds(pl.multiple_of(k * chunk, chunk), chunk)
        finish(YN, k * chunk, chunk)
        finish(XN, half + k * chunk, chunk)
        send_x(0, k).wait_recv()
        acc[at_y, :] = acc[at_y, :] + rx[0, here, :]
        send_y(2, k).start()
        send_y(0, k).wait_recv()
        acc[at_x, :] = acc[at_x, :] + ry[0, here, :]
        send_x(2, k).start()
        return carry

    lax.fori_loop(0, n_chunk, passed_step, 0)
    finish(OWN, 0, rows)

    def direct_add(k, carry):
        here = pl.ds(pl.multiple_of(k * chunk, chunk), chunk)
        there = pl.ds(pl.multiple_of(half + k * chunk, chunk), chunk)
        send_x(1, k).wait_recv()
        acc[here, :] = acc[here, :] + rx[1, here, :]
        send_y(1, k).wait_recv()
        acc[there, :] = acc[there, :] + ry[1, here, :]
        return carry

    lax.fori_loop(0, n_chunk, direct_add, 0)

    def last_add(k, carry):
        here = pl.ds(pl.multiple_of(k * chunk, chunk), chunk)
        there = pl.ds(pl.multiple_of(half + k * chunk, chunk), chunk)
        send_y(2, k).wait_recv()
        out_ref[here, :] = (tok[here, :].astype(jnp.float32) + (acc[here, :] + ry[2, here, :])).astype(out_ref.dtype)
        send_x(2, k).wait_recv()
        out_ref[there, :] = (tok[there, :].astype(jnp.float32) + (acc[there, :] + rx[2, here, :])).astype(out_ref.dtype)
        return carry

    lax.fori_loop(0, n_chunk, last_add, 0)

    def drain_w(i, carry):
        for m in range(3):
            send_w(m, i).wait_send()
            partner_own(m, i).wait_send()
            partner_fwd(m, i).wait_send()
        return carry

    lax.fori_loop(0, n_own, drain_w, 0)

    def drain_c(k, carry):
        for kind in range(3):
            send_x(kind, k).wait_send()
            send_y(kind, k).wait_send()
        return carry

    lax.fori_loop(0, n_chunk, drain_c, 0)
    for cp in (tok_x, tok_y, tok_d, *g_copies):
        cp.wait_send()


def solution(mesh):
    ep_size = mesh.shape["ep"]
    row_spec = P(("rep", "ep", "fsdp"), None)

    def device_step(tokens, expert_idx, gates, w_gate, w_up, w_down):
        rows, top_k = expert_idx.shape
        n_local, half_w, ffn = w_gate.shape
        width = tokens.shape[1]
        n_own = n_local // 2
        num_experts = n_local * ep_size
        capacity = (2 * rows * top_k + num_experts - 1) // num_experts
        half = rows // 2
        chunk = 64
        n_chunk = half // chunk
        dma = pltpu.SemaphoreType.DMA
        hbm = pl.BlockSpec(memory_space=pl.ANY)
        vmem = pl.BlockSpec(memory_space=pltpu.VMEM)
        return pl.pallas_call(
            functools.partial(moe_kernel, num_experts, capacity, chunk),
            out_shape=jax.ShapeDtypeStruct((rows, width), jnp.bfloat16),
            in_specs=[hbm, vmem, vmem, hbm, hbm, hbm],
            out_specs=vmem,
            scratch_shapes=[
                pltpu.VMEM((4 * rows, width), jnp.bfloat16),
                pltpu.VMEM((3, n_local, 2, half_w, ffn), jnp.bfloat16),
                pltpu.VMEM((4 * rows, width), jnp.float32),
                pltpu.VMEM((2, 4 * rows, ffn), jnp.bfloat16),
                pltpu.VMEM((128, rows), jnp.float32),
                pltpu.VMEM((3, n_local, rows), jnp.float32),
                pltpu.VMEM((4, rows, 128), jnp.float32),
                pltpu.VMEM((3, half, width), jnp.float32),
                pltpu.VMEM((3, half, width), jnp.float32),
                dma, dma((3,)), dma((3,)), dma((3,)), dma((3,)),
                dma((3, n_own)), dma((3, n_own)), dma((3, n_own)),
                dma((3, n_own)), dma((3, n_own)), dma((3, n_own)), dma((3, n_own)),
                dma((3, n_chunk)), dma((3, n_chunk)), dma((3, n_chunk)), dma((3, n_chunk)),
            ],
            compiler_params=pltpu.CompilerParams(collective_id=0, has_side_effects=True, vmem_limit_bytes=67_043_328),
        )(tokens, expert_idx, gates, w_gate, w_up, w_down)

    return jax.shard_map(device_step, mesh=mesh, in_specs=(row_spec, row_spec, row_spec, P("ep", "fsdp", None), P("ep", "fsdp", None), P("ep", None, "fsdp")), out_specs=row_spec, check_vma=False)
```

time: 639 us -> 243 us (0.38)
  waiting for transfers between devices: 383 us -> 0 us
  Pallas kernels: 0 us -> 237 us
  matrix products: 140 us -> 0 us
  other arithmetic: 70.8 us -> 0 us
  starting transfers between devices: 15.2 us -> 0 us
  between operations: 13.2 us -> 0.01 us
  local copies, waits for them, and re-layouts: 16.2 us -> 5.38 us
    all_to_all x2 -> x0, waiting for transfers between devices: 354 us -> none  [the longest x1 182 us: device_step(): back_buf = lax.all_to_all(expert_out, 'ep', 0, 0, tiled=True)]
    pallas_call x0 -> x1, Pallas kernels: none -> 237 us  [device_step(): pl.pallas_call(functools.partial(moe_kernel, num_experts, capacity, chunk...]
    dot_general x4 -> x0, matrix products: 140 us -> none  [the longest x1 77.6 us: device_step(): jnp.einsum('tkf,fd->tkd', select, back_rows, preferred_element_type=jnp.f...]
    reduce_sum x2 -> x0, other arithmetic: 59 us -> none  [the longest x1 58.6 us: device_step(): jnp.einsum('tkf,td->fd', select, tokens, preferred_element_type=jnp.float32)]
    all_gather x3 -> x0, waiting for transfers between devices: 26.8 us -> none  [the longest x1 17.5 us: device_step(): wd_full = lax.all_gather(w_down, 'fsdp', axis=2, tiled=True)]
    all_to_all x2 -> x0, starting transfers between devices: 15 us -> none  [the longest x1 7.97 us: device_step(): back_buf = lax.all_to_all(expert_out, 'ep', 0, 0, tiled=True)]
    convert_element_type x1 -> x0, local copies, waits for them, and re-layouts: 13.9 us -> none  [device_step(): jnp.einsum('sncf,nfd->sncd', hidden, wd_full, preferred_element_type=jnp....]
    another operation x3 -> x0, other arithmetic: 9.62 us -> none
  transfers between devices with their start and end apart: 5 -> 0, of which waited for: 4 -> 0; matrix products, arithmetic and copies ran while one was open for 17% -> 0% of each run, Pallas kernels for 0% -> 0%
where the time goes in v1:
time: 243 us
  Pallas kernels  237 us (98%)
  local copies, waits for them, and re-layouts  5.38 us (2%)
    pallas_call x1, Pallas kernels, device_step(): pl.pallas_call(functools.partial(moe_kernel, num_experts, capacity, chunk...  237 us
    unnamed x3, local copies, waits for them, and re-layouts  5.38 us

profile of v1, /device:TPU:1, one launch (start us, length us, event | category | flops | bytes accessed | tf_op | source)
XLA Modules:
  0.0 242.9 jit_solution(2726578488607006085)
XLA Ops:
  0.0 1.6 copy.7.idx_ref
  1.6 1.6 copy.8.gates_ref
  3.1 237.5 %shard_map.64 = bf16[512,1024]{1,0:T(8,128)(2,1)} custom-call(bf16[512,1024]{1,0:T(8,128)(2,1)} %tokens_hbm.1, s32[512,8]{1,0:T(8,128)} %copy.7.idx_ref, f32[512,8]{1,0:T(8,128)} %copy.8.gates_ref, bf16[8,512,512]{2,1,0:T(8,128)(2,1)} %wg_hbm.1, bf16[8,512,512]{2,1,0:T(8,128)(2,1)} %wu_hbm.1, bf16[8,512,512]{2,1,0:T(8,128)(2,1)} %wd_hbm.1), custom_call_target="tpu_custom_call" | custom-call | tf_op jit(solution)/shard_map/pallas_call | solution.py:291
  240.6 2.3 copy.10

commit v2 on v1

v2 whole, which is shorter than its diff:
```python
import functools

import jax
import jax.numpy as jnp
from jax import lax
from jax.experimental import pallas as pl
from jax.experimental.pallas import tpu as pltpu
from jax.sharding import PartitionSpec as P

MESH = pl.DeviceIdType.MESH
OWN, XN, YN, DG = 0, 1, 2, 3


def moe_kernel(num_experts, capacity, chunk, tokens_hbm, idx_ref, gates_ref, wg_hbm, wu_hbm, wd_hbm, out_ref,
               tok, w, acc, hid, gt_send, gt_recv, gcol, rx, ry,
               loc_tok_sem, tok_send, tok_recv, g_send, g_recv_sem, loc_sem, ys_sem, yr_sem,
               po_s, po_r, pf_s, pf_r, cx_s, cx_r, cy_s, cy_r):
    rows, width = out_ref.shape
    n_local = wg_hbm.shape[0]
    n_own = n_local // 2
    half_w = width // 2
    n_chunk = rows // chunk
    ep = lax.axis_index("ep")
    y = lax.axis_index("fsdp")
    c = lax.rem(ep, 2)
    x = ep // 2
    oy = 1 - y
    x_dev = {"ep": lax.rem(ep + 2, 4), "fsdp": y}
    y_dev = {"ep": ep, "fsdp": oy}
    d_dev = {"ep": lax.rem(ep + 2, 4), "fsdp": oy}
    p_dev = {"ep": ep + 1 - 2 * c, "fsdp": y}
    w_hbm = (wg_hbm, wu_hbm, wd_hbm)

    def remote(src, dst, s, r, dev):
        return pltpu.make_async_remote_copy(src_ref=src, dst_ref=dst, send_sem=s, recv_sem=r, device_id=dev, device_id_type=MESH)

    def span(start, n):
        return pl.ds(pl.multiple_of(start, chunk), n)

    def block(b):
        return tok.at[pl.ds(b * rows, rows)]

    barrier = pltpu.get_barrier_semaphore()
    for dev in (x_dev, y_dev, d_dev, p_dev):
        pl.semaphore_signal(barrier, inc=1, device_id=dev, device_id_type=MESH)
    pl.semaphore_wait(barrier, 4)

    tok_y = remote(tokens_hbm, block(YN), tok_send.at[0], tok_recv.at[0], y_dev)
    tok_x = remote(tokens_hbm, block(XN), tok_send.at[1], tok_recv.at[1], x_dev)
    tok_d = remote(block(YN), block(DG), tok_send.at[2], tok_recv.at[2], x_dev)
    tok_l = pltpu.make_async_copy(tokens_hbm, block(OWN), loc_tok_sem)
    tok_y.start()
    tok_x.start()
    tok_l.start()

    row = lax.broadcasted_iota(jnp.int32, (num_experts, 1), 0)
    dest, slot = row // n_local, lax.rem(row, n_local)
    dx, dy = lax.rem(dest, 2), dest // 2
    ex = x + dx - 2 * x * dx
    ey = y + dy - 2 * y * dy
    sc = slot // n_own
    ec = c + sc - 2 * c * sc
    expert = (2 * ex + ec) * n_local + ey * n_own + lax.rem(slot, n_own)
    dense = jnp.zeros((num_experts, rows), jnp.float32)
    chosen = jnp.zeros((num_experts, rows), jnp.float32)
    for j in range(idx_ref.shape[0]):
        hit = idx_ref[j:j + 1, :] == expert
        dense = jnp.where(hit, gates_ref[j:j + 1, :], dense)
        chosen = jnp.where(hit, 1.0, chosen)
    before = lax.broadcasted_iota(jnp.int32, (rows, rows), 0) < lax.broadcasted_iota(jnp.int32, (rows, rows), 1)
    taken = jnp.dot(chosen.astype(jnp.bfloat16), before.astype(jnp.bfloat16), preferred_element_type=jnp.float32)
    dense = jnp.where(taken < float(capacity), dense, 0.0)
    gt_send[...] = dense
    g_copies = []
    for k, (b, dev) in enumerate(((XN, x_dev), (YN, y_dev), (DG, d_dev))):
        cp = remote(gt_send.at[pl.ds(b * n_local, n_local)], gt_recv.at[k], g_send.at[k], g_recv_sem.at[k], dev)
        cp.start()
        g_copies.append(cp)

    def local_w(m, i):
        return pltpu.make_async_copy(w_hbm[m].at[y * n_own + i], w.at[m, i, y], loc_sem.at[m, i])

    def send_w(m, i):
        return remote(w_hbm[m].at[oy * n_own + i], w.at[m, i, y], ys_sem.at[m, i], yr_sem.at[m, i], y_dev)

    def arrived_w(m, i):
        return remote(w_hbm[m].at[oy * n_own + i], w.at[m, i, oy], ys_sem.at[m, i], yr_sem.at[m, i], y_dev)

    def partner_own(m, i):
        return remote(w_hbm[m].at[y * n_own + i], w.at[m, n_own + i, y], po_s.at[m, i], po_r.at[m, i], p_dev)

    def partner_fwd(m, i):
        return remote(w.at[m, i, oy], w.at[m, n_own + i, oy], pf_s.at[m, i], pf_r.at[m, i], p_dev)

    for i in range(n_own):
        for m in range(2):
            send_w(m, i).start()
    for i in range(n_own):
        send_w(2, i).start()
    for i in range(n_own):
        for m in range(3):
            local_w(m, i).start()
            partner_own(m, i).start()

    def clear(k, carry):
        for part in range(2):
            acc[part, span(k * chunk, chunk), :] = jnp.zeros((chunk, half_w), jnp.float32)
        return carry

    lax.fori_loop(0, 4 * n_chunk, clear, 0)

    def column_gates(b, g):
        gcol[pl.ds(b * rows, rows), :] = jnp.concatenate([g, jnp.zeros((128 - n_local, rows), jnp.float32)], axis=0).T

    column_gates(OWN, gt_send[0:n_local, :])
    tok_y.wait_recv()
    tok_d.start()
    for k, b in enumerate((XN, YN, DG)):
        g_copies[k].wait_recv()
        column_gates(b, gt_recv[k])

    tok_l.wait()
    tok_x.wait_recv()
    tok_d.wait_recv()

    lane = lax.broadcasted_iota(jnp.int32, (1, 128), 1)

    def gate_up(s, start, n):
        at = span(start, n)
        r = tok[at, :]
        a = jnp.dot(r, w[0, s].reshape(width, w.shape[-1]), preferred_element_type=jnp.float32)
        u = jnp.dot(r, w[1, s].reshape(width, w.shape[-1]), preferred_element_type=jnp.float32)
        hid[s, at, :] = (a * jax.nn.sigmoid(a) * u).astype(jnp.bfloat16)

    def weighted(s, start, n, part):
        at = span(start, n)
        g = jnp.sum(jnp.where(lane == s, gcol[at, :], 0.0), axis=1, keepdims=True)
        o = jnp.dot(hid[s, at, :], w[2, s, part], preferred_element_type=jnp.float32).astype(jnp.bfloat16).astype(jnp.float32)
        return jnp.where(g != 0.0, g * o, 0.0)

    def down(s, part):
        def step(b, carry):
            at = span(b * rows, rows)
            acc[part, at, :] = acc[part, at, :] + weighted(s, b * rows, rows, part)
            return carry

        lax.fori_loop(0, 4, step, 0)

    def arrive(m, i):
        arrived_w(m, i).wait_recv()
        partner_fwd(m, i).start()

    def round_one(i, carry):
        for m in range(2):
            arrive(m, i)
            local_w(m, i).wait()
        local_w(2, i).wait()

        def both(s):
            def step(b, carry):
                at = span(b * rows, rows)
                gate_up(s, b * rows, rows)
                acc[y, at, :] = acc[y, at, :] + weighted(s, b * rows, rows, y)
                return carry

            lax.fori_loop(0, 4, step, 0)

        both(i)
        for m in range(2):
            partner_own(m, i).wait_recv()
            partner_fwd(m, i).wait_recv()
        partner_own(2, i).wait_recv()
        both(n_own + i)
        return carry

    lax.fori_loop(0, n_own - 1, round_one, 0)

    last = n_own - 1
    tile = 2 * chunk
    n_tile = rows // tile

    def tile_of(part, b, k):
        return acc.at[part, span(b * rows + k * tile, tile)]

    def send_x(kind, k):
        part = y if kind < 2 else oy
        return remote(tile_of(part, (DG, XN)[kind % 2], k), rx.at[kind, span(k * tile, tile)], cx_s.at[kind, k], cx_r.at[kind, k], x_dev)

    def send_y(kind, k):
        part = y if kind == 0 else oy
        return remote(tile_of(part, YN, k), ry.at[kind, span(k * tile, tile)], cy_s.at[kind, k], cy_r.at[kind, k], y_dev)

    def add_tile(part, b, k, got):
        at = span(b * rows + k * tile, tile)
        acc[part, at, :] = acc[part, at, :] + got[span(k * tile, tile), :]

    def finish(part, start, n):
        at = span(start, n)
        acc[part, at, :] = (acc[part, at, :] + weighted(last, start, n, part)) + weighted(n_own + last, start, n, part)

    for m in range(2):
        arrive(m, last)
        local_w(m, last).wait()
    local_w(2, last).wait()
    for m in range(2):
        partner_own(m, last).wait_recv()
        partner_fwd(m, last).wait_recv()
    partner_own(2, last).wait_recv()

    def close_one(b, k, n):
        start = b * rows + k * n
        gate_up(last, start, n)
        gate_up(n_own + last, start, n)
        finish(y, start, n)

    for kind, b in enumerate((DG, XN)):
        def step(k, carry, kind=kind, b=b):
            close_one(b, k, tile)
            send_x(kind, k).start()
            return carry

        lax.fori_loop(0, n_tile, step, 0)
    close_one(YN, 0, rows)
    close_one(OWN, 0, rows)

    def round_two(i, carry):
        arrive(2, i)
        down(i, oy)
        partner_fwd(2, i).wait_recv()
        down(n_own + i, oy)
        return carry

    lax.fori_loop(0, n_own - 1, round_two, 0)

    def pass_one(k, carry):
        send_x(0, k).wait_recv()
        add_tile(y, YN, k, rx.at[0])
        send_y(0, k).start()
        return carry

    lax.fori_loop(0, n_tile, pass_one, 0)

    arrive(2, last)
    partner_fwd(2, last).wait_recv()
    for kind, b in ((2, DG), (3, XN)):
        def step(k, carry, kind=kind, b=b):
            finish(oy, b * rows + k * tile, tile)
            send_x(kind, k).start()
            return carry

        lax.fori_loop(0, n_tile, step, 0)
    finish(oy, YN * rows, rows)
    finish(oy, OWN * rows, rows)

    def pass_two(k, carry):
        send_x(2, k).wait_recv()
        add_tile(oy, YN, k, rx.at[2])
        send_y(1, k).start()
        return carry

    lax.fori_loop(0, n_tile, pass_two, 0)

    def add_first(k, carry):
        send_x(1, k).wait_recv()
        add_tile(y, OWN, k, rx.at[1])
        send_y(0, k).wait_recv()
        add_tile(oy, OWN, k, ry.at[0])
        return carry

    lax.fori_loop(0, n_tile, add_first, 0)

    def last_add(k, carry):
        at = span(k * tile, tile)
        send_y(1, k).wait_recv()
        acc[y, at, :] = acc[y, at, :] + ry[1, at, :]
        send_x(3, k).wait_recv()
        acc[oy, at, :] = acc[oy, at, :] + rx[3, at, :]
        for part in range(2):
            cols = pl.ds(part * half_w, half_w)
            out_ref[at, cols] = (tok[at, cols].astype(jnp.float32) + acc[part, at, :]).astype(out_ref.dtype)
        return carry

    lax.fori_loop(0, n_tile, last_add, 0)

    def drain_w(i, carry):
        for m in range(3):
            send_w(m, i).wait_send()
            partner_own(m, i).wait_send()
            partner_fwd(m, i).wait_send()
        return carry

    lax.fori_loop(0, n_own, drain_w, 0)

    def drain_c(k, carry):
        for kind in range(4):
            send_x(kind, k).wait_send()
        for kind in range(2):
            send_y(kind, k).wait_send()
        return carry

    lax.fori_loop(0, n_tile, drain_c, 0)
    for cp in (tok_x, tok_y, tok_d, *g_copies):
        cp.wait_send()


def solution(mesh):
    ep_size = mesh.shape["ep"]
    row_spec = P(("rep", "ep", "fsdp"), None)

    def device_step(tokens, expert_idx, gates, w_gate, w_up, w_down):
        rows, top_k = expert_idx.shape
        n_local, half_w, ffn = w_gate.shape
        width = tokens.shape[1]
        n_own = n_local // 2
        num_experts = n_local * ep_size
        capacity = (2 * rows * top_k + num_experts - 1) // num_experts
        chunk = 64
        n_tile = rows // (2 * chunk)
        dma = pltpu.SemaphoreType.DMA
        hbm = pl.BlockSpec(memory_space=pl.ANY)
        vmem = pl.BlockSpec(memory_space=pltpu.VMEM)
        return pl.pallas_call(
            functools.partial(moe_kernel, num_experts, capacity, chunk),
            out_shape=jax.ShapeDtypeStruct((rows, width), jnp.bfloat16),
            in_specs=[hbm, vmem, vmem, hbm, hbm, hbm],
            out_specs=vmem,
            scratch_shapes=[
                pltpu.VMEM((4 * rows, width), jnp.bfloat16),
                pltpu.VMEM((3, n_local, 2, half_w, ffn), jnp.bfloat16),
                pltpu.VMEM((2, 4 * rows, half_w), jnp.float32),
                pltpu.VMEM((n_local, 4 * rows, ffn), jnp.bfloat16),
                pltpu.VMEM((num_experts, rows), jnp.float32),
                pltpu.VMEM((3, n_local, rows), jnp.float32),
                pltpu.VMEM((4 * rows, 128), jnp.float32),
                pltpu.VMEM((4, rows, half_w), jnp.float32),
                pltpu.VMEM((2, rows, half_w), jnp.float32),
                dma, dma((3,)), dma((3,)), dma((3,)), dma((3,)),
                dma((3, n_own)), dma((3, n_own)), dma((3, n_own)),
                dma((3, n_own)), dma((3, n_own)), dma((3, n_own)), dma((3, n_own)),
                dma((4, n_tile)), dma((4, n_tile)), dma((2, n_tile)), dma((2, n_tile)),
            ],
            compiler_params=pltpu.CompilerParams(collective_id=0, has_side_effects=True, vmem_limit_bytes=67_043_328),
        )(tokens, expert_idx.T, gates.T, w_gate, w_up, w_down)

    return jax.shard_map(device_step, mesh=mesh, in_specs=(row_spec, row_spec, row_spec, P("ep", "fsdp", None), P("ep", "fsdp", None), P("ep", None, "fsdp")), out_specs=row_spec, check_vma=False)
```

time: 243 us -> 218 us (0.90)
  Pallas kernels: 237 us -> 215 us
  local copies, waits for them, and re-layouts: 5.38 us -> 2.26 us
    pallas_call x1, Pallas kernels: 237 us -> 215 us  [device_step(): pl.pallas_call(functools.partial(moe_kernel, num_experts, capacity, chunk...]
    unnamed x3 -> x1, local copies, waits for them, and re-layouts: 5.38 us -> 2.26 us
where the time goes in v2:
time: 218 us; the launch traced here: 217 us
  Pallas kernels  215 us (99%)
  local copies, waits for them, and re-layouts  2.26 us (1%)
    pallas_call x1, Pallas kernels, device_step(): pl.pallas_call(functools.partial(moe_kernel, num_experts, capacity, chunk...  215 us

profile of v2, /device:TPU:1, one launch (start us, length us, event | category | flops | bytes accessed | tf_op | source)
XLA Modules:
  0.0 216.9 jit_solution(1723027305467887210)
XLA Ops:
  0.0 214.6 %shard_map.64 = bf16[512,1024]{1,0:T(8,128)(2,1)} custom-call(bf16[512,1024]{1,0:T(8,128)(2,1)} %tokens_hbm.1, s32[8,512]{1,0:T(8,128)} %bitcast.2, f32[8,512]{1,0:T(8,128)} %bitcast.3, bf16[8,512,512]{2,1,0:T(8,128)(2,1)} %wg_hbm.1, bf16[8,512,512]{2,1,0:T(8,128)(2,1)} %wu_hbm.1, bf16[8,512,512]{2,1,0:T(8,128)(2,1)} %wd_hbm.1), custom_call_target="tpu_custom_call" | custom-call | tf_op jit(solution)/shard_map/pallas_call | solution.py:322
  214.6 2.3 %copy.8 = bf16[512,1024]{1,0:T(8,128)(2,1)} copy(bf16[512,1024]{1,0:T(8,128)(2,1)} %shard_map.64) | data formatting | bytes 2097152

commit v3 on v2

v3 whole, which is shorter than its diff:
```python
import functools

import jax
import jax.numpy as jnp
from jax import lax
from jax.experimental import pallas as pl
from jax.experimental.pallas import tpu as pltpu
from jax.sharding import PartitionSpec as P

MESH = pl.DeviceIdType.MESH
OWN, XN, YN, DG = 0, 1, 2, 3


def moe_kernel(num_experts, capacity, chunk, spill_rows, tokens_hbm, idx_hbm, gates_hbm, wg_hbm, wu_hbm, wd_hbm, out_hbm,
               idx_ref, gates_ref, tok, w, acc, hid, gt_send, gt_recv, gcol, rx, ry, ry_spill,
               small_sem, out_sem, loc_tok_sem, tok_send, tok_recv, g_send, g_recv_sem, loc_sem, ys_sem, yr_sem,
               po_s, po_r, pf_s, pf_r, ds_sem, dr_sem, df_s, df_r, cx_s, cx_r, cy_s, cy_r, spill_s, spill_r):
    rows, width = out_hbm.shape
    n_local = wg_hbm.shape[0]
    n_own = n_local // 2
    half_w = width // 2
    group = half_w // 2
    n_chunk = rows // chunk
    ep = lax.axis_index("ep")
    y = lax.axis_index("fsdp")
    c = lax.rem(ep, 2)
    x = ep // 2
    oy = 1 - y
    x_dev = {"ep": lax.rem(ep + 2, 4), "fsdp": y}
    y_dev = {"ep": ep, "fsdp": oy}
    p_dev = {"ep": ep + 1 - 2 * c, "fsdp": y}
    w_hbm = (wg_hbm, wu_hbm, wd_hbm)

    def remote(src, dst, s, r, dev):
        return pltpu.make_async_remote_copy(src_ref=src, dst_ref=dst, send_sem=s, recv_sem=r, device_id=dev, device_id_type=MESH)

    def span(start, n):
        return pl.ds(pl.multiple_of(start, 16), n)

    def block(b):
        return tok.at[pl.ds(b * rows, rows)]

    idx_in = pltpu.make_async_copy(idx_hbm, idx_ref, small_sem.at[0])
    gates_in = pltpu.make_async_copy(gates_hbm, gates_ref, small_sem.at[1])
    idx_in.start()
    gates_in.start()
    barrier = pltpu.get_barrier_semaphore()
    for dev in (y_dev, x_dev, p_dev):
        pl.semaphore_signal(barrier, inc=1, device_id=dev, device_id_type=MESH)
    pl.semaphore_wait(barrier, 3)

    tok_y = remote(tokens_hbm, block(YN), tok_send.at[0], tok_recv.at[0], y_dev)
    tok_x = remote(tokens_hbm, block(XN), tok_send.at[1], tok_recv.at[1], x_dev)
    tok_d = remote(block(YN), block(DG), tok_send.at[2], tok_recv.at[2], x_dev)
    tok_l = pltpu.make_async_copy(tokens_hbm, block(OWN), loc_tok_sem)
    tok_y.start()
    tok_x.start()
    tok_l.start()

    row = lax.broadcasted_iota(jnp.int32, (num_experts, 1), 0)
    dest, slot = row // n_local, lax.rem(row, n_local)
    dx, dy = lax.rem(dest, 2), dest // 2
    ex = x + dx - 2 * x * dx
    ey = y + dy - 2 * y * dy
    sc = slot // n_own
    ec = c + sc - 2 * c * sc
    expert = (2 * ex + ec) * n_local + ey * n_own + lax.rem(slot, n_own)
    idx_in.wait()
    gates_in.wait()
    dense = jnp.zeros((num_experts, rows), jnp.float32)
    chosen = jnp.zeros((num_experts, rows), jnp.float32)
    for j in range(idx_ref.shape[0]):
        hit = idx_ref[j:j + 1, :] == expert
        dense = jnp.where(hit, gates_ref[j:j + 1, :], dense)
        chosen = jnp.where(hit, 1.0, chosen)
    before = lax.broadcasted_iota(jnp.int32, (rows, rows), 0) < lax.broadcasted_iota(jnp.int32, (rows, rows), 1)
    taken = jnp.dot(chosen.astype(jnp.bfloat16), before.astype(jnp.bfloat16), preferred_element_type=jnp.float32)
    dense = jnp.where(taken < float(capacity), dense, 0.0)
    gt_send[...] = dense
    g_x = remote(gt_send.at[pl.ds(XN * n_local, n_local)], gt_recv.at[pl.ds(0, n_local)], g_send.at[0], g_recv_sem.at[0], x_dev)
    g_y = remote(gt_send.at[pl.ds(YN * n_local, 2 * n_local)], gt_recv.at[pl.ds(n_local, 2 * n_local)], g_send.at[1], g_recv_sem.at[1], y_dev)
    g_d = remote(gt_recv.at[pl.ds(2 * n_local, n_local)], gt_recv.at[pl.ds(3 * n_local, n_local)], g_send.at[2], g_recv_sem.at[2], x_dev)
    g_y.start()
    g_x.start()

    def local_w(m, i):
        return pltpu.make_async_copy(w_hbm[m].at[y * n_own + i], w.at[m, i, y], loc_sem.at[m, i])

    def send_w(m, i):
        return remote(w_hbm[m].at[oy * n_own + i], w.at[m, i, y], ys_sem.at[m, i], yr_sem.at[m, i], y_dev)

    def arrived_w(m, i):
        return remote(w_hbm[m].at[oy * n_own + i], w.at[m, i, oy], ys_sem.at[m, i], yr_sem.at[m, i], y_dev)

    def partner_own(m, i):
        return remote(w_hbm[m].at[y * n_own + i], w.at[m, n_own + i, y], po_s.at[m, i], po_r.at[m, i], p_dev)

    def partner_fwd(m, i):
        return remote(w.at[m, i, oy], w.at[m, n_own + i, oy], pf_s.at[m, i], pf_r.at[m, i], p_dev)

    def down_half(slot, part, g):
        return w.at[2, slot, part, :, pl.ds(g * group, group)]

    def send_d(g, i):
        return remote(wd_hbm.at[oy * n_own + i, :, pl.ds(g * group, group)], down_half(i, y, g), ds_sem.at[g, i], dr_sem.at[g, i], y_dev)

    def arrived_d(g, i):
        return remote(wd_hbm.at[oy * n_own + i, :, pl.ds(g * group, group)], down_half(i, oy, g), ds_sem.at[g, i], dr_sem.at[g, i], y_dev)

    def fwd_d(g, i):
        return remote(down_half(i, oy, g), down_half(n_own + i, oy, g), df_s.at[g, i], df_r.at[g, i], p_dev)

    for i in range(n_own):
        for m in range(2):
            send_w(m, i).start()
    for g in range(2):
        for i in range(n_own):
            send_d(g, i).start()
    for i in range(n_own):
        for m in range(3):
            local_w(m, i).start()
            partner_own(m, i).start()

    def clear(k, carry):
        for part in range(2):
            acc[part, span(k * chunk, chunk), :] = jnp.zeros((chunk, half_w), jnp.float32)
        return carry

    lax.fori_loop(0, 4 * n_chunk, clear, 0)

    def column_gates(b, g):
        gcol[pl.ds(b * rows, rows), :] = jnp.concatenate([g, jnp.zeros((128 - n_local, rows), jnp.float32)], axis=0).T

    column_gates(OWN, gt_send[0:n_local, :])
    tok_y.wait_recv()
    tok_d.start()
    g_y.wait_recv()
    g_d.start()
    for k, (b, cp) in enumerate(((XN, g_x), (YN, None), (None, None), (DG, g_d))):
        if cp is not None:
            cp.wait_recv()
        if b is not None:
            column_gates(b, gt_recv[k * n_local:(k + 1) * n_local, :])

    tok_l.wait()
    tok_x.wait_recv()
    tok_d.wait_recv()

    lane = lax.broadcasted_iota(jnp.int32, (1, 128), 1)

    def gate_up(s, start, n):
        at = span(start, n)
        r = tok[at, :]
        a = jnp.dot(r, w[0, s].reshape(width, w.shape[-1]), preferred_element_type=jnp.float32)
        u = jnp.dot(r, w[1, s].reshape(width, w.shape[-1]), preferred_element_type=jnp.float32)
        hid[s, at, :] = (a * jax.nn.sigmoid(a) * u).astype(jnp.bfloat16)

    def weighted(s, start, n, part, col=0, n_col=half_w):
        at = span(start, n)
        g = jnp.sum(jnp.where(lane == s, gcol[at, :], 0.0), axis=1, keepdims=True)
        o = jnp.dot(hid[s, at, :], w[2, s, part, :, pl.ds(col, n_col)], preferred_element_type=jnp.float32).astype(jnp.bfloat16).astype(jnp.float32)
        return jnp.where(g != 0.0, g * o, 0.0)

    def down(s, g):
        cols = pl.ds(g * group, group)

        def step(b, carry):
            at = span(b * rows, rows)
            acc[oy, at, cols] = acc[oy, at, cols] + weighted(s, b * rows, rows, oy, g * group, group)
            return carry

        lax.fori_loop(0, 4, step, 0)

    def arrive(m, i):
        arrived_w(m, i).wait_recv()
        partner_fwd(m, i).start()

    def round_one(i, carry):
        for m in range(2):
            arrive(m, i)
            local_w(m, i).wait()
        local_w(2, i).wait()

        def both(s):
            def step(b, carry):
                at = span(b * rows, rows)
                gate_up(s, b * rows, rows)
                acc[y, at, :] = acc[y, at, :] + weighted(s, b * rows, rows, y)
                return carry

            lax.fori_loop(0, 4, step, 0)

        both(i)
        for m in range(2):
            partner_own(m, i).wait_recv()
            partner_fwd(m, i).wait_recv()
        partner_own(2, i).wait_recv()
        both(n_own + i)
        return carry

    lax.fori_loop(0, n_own - 1, round_one, 0)

    last = n_own - 1
    tile = 2 * chunk
    n_tile = rows // tile
    kept = rows - spill_rows
    starts = [0, tile // 2, *range(tile, kept, tile)]
    pieces = [(a, b - a) for a, b in zip(starts, [*starts[1:], kept])]
    n_first = len(pieces)

    def part_of(part, b, start, n):
        return acc.at[part, span(b * rows + start, n)]

    def send_x(kind, k):
        start, n = pieces[k] if kind == 0 else (k * tile, tile)
        return remote(part_of(y, (DG, XN)[kind], start, n), rx.at[kind, span(start, n)], cx_s.at[kind, k], cx_r.at[kind, k], x_dev)

    def send_xg(kind, g, k):
        cols = pl.ds(g * group, group)
        sem = 2 + 2 * kind + g
        return remote(acc.at[oy, span((DG, XN)[kind] * rows + k * tile, tile), cols], rx.at[2 + kind, span(k * tile, tile), cols],
                      cx_s.at[sem, k], cx_r.at[sem, k], x_dev)

    def send_y(k):
        return remote(part_of(y, YN, k * tile, tile), ry.at[0, span(k * tile, tile)], cy_s.at[0, k], cy_r.at[0, k], y_dev)

    def send_yg(g, k):
        cols = pl.ds(g * group, group)
        return remote(acc.at[oy, span(YN * rows + k * tile, tile), cols], ry.at[1, span(k * tile, tile), cols],
                      cy_s.at[1 + g, k], cy_r.at[1 + g, k], y_dev)

    spill = remote(part_of(y, DG, kept, spill_rows), ry_spill, spill_s, spill_r, y_dev)

    def add_rows(part, b, start, n, got, col=0, n_col=half_w):
        at, cols = span(b * rows + start, n), pl.ds(col, n_col)
        acc[part, at, cols] = acc[part, at, cols] + got[:, cols]

    def finish(part, start, n, col=0, n_col=half_w):
        at, cols = span(start, n), pl.ds(col, n_col)
        first = acc[part, at, cols] + weighted(last, start, n, part, col, n_col)
        acc[part, at, cols] = first + weighted(n_own + last, start, n, part, col, n_col)

    for m in range(2):
        arrive(m, last)
        local_w(m, last).wait()
    local_w(2, last).wait()
    for m in range(2):
        partner_own(m, last).wait_recv()
        partner_fwd(m, last).wait_recv()
    partner_own(2, last).wait_recv()

    def close_one(b, start, n):
        start = b * rows + start
        gate_up(last, start, n)
        gate_up(n_own + last, start, n)
        finish(y, start, n)

    def x_one(k, carry):
        close_one(XN, k * tile, tile)
        send_x(1, k).start()
        return carry

    for k, (start, n) in enumerate(pieces):
        close_one(DG, start, n)
        send_x(0, k).start()
    close_one(DG, kept, spill_rows)
    spill.start()
    lax.fori_loop(0, n_tile, x_one, 0)
    close_one(YN, 0, rows)
    close_one(OWN, 0, rows)

    def arrive_d(g, i):
        arrived_d(g, i).wait_recv()
        fwd_d(g, i).start()

    def round_two(i, carry, g=0):
        arrive_d(g, i)
        down(i, g)
        fwd_d(g, i).wait_recv()
        down(n_own + i, g)
        return carry

    def close_two(g, b):
        finish(oy, b * rows, rows, g * group, group)

    lax.fori_loop(0, n_own - 1, functools.partial(round_two, g=0), 0)
    arrive_d(0, last)
    fwd_d(0, last).wait_recv()

    def diag_two(k, carry, g=0):
        finish(oy, DG * rows + k * tile, tile, g * group, group)
        send_xg(0, g, k).start()
        return carry

    lax.fori_loop(0, n_tile, functools.partial(diag_two, g=0), 0)
    for b in (XN, YN, OWN):
        close_two(0, b)

    for k, (start, n) in enumerate(pieces):
        send_x(0, k).wait_recv()
        add_rows(y, YN, start, n, rx.at[0, span(start, n)])
        if k > 0:
            send_y(k - 1).start()

    lax.fori_loop(0, n_own - 1, functools.partial(round_two, g=1), 0)
    arrive_d(1, last)
    fwd_d(1, last).wait_recv()
    lax.fori_loop(0, n_tile, functools.partial(diag_two, g=1), 0)
    spill.wait_recv()
    add_rows(oy, XN, kept, spill_rows, ry_spill)
    for k in range(n_tile):
        send_xg(1, 0, k).start()

    def x_two(k, carry):
        finish(oy, XN * rows + k * tile, tile, group, group)
        send_xg(1, 1, k).start()
        return carry

    lax.fori_loop(0, n_tile, x_two, 0)
    close_two(1, YN)
    for g in range(2):
        def pass_two(k, carry, g=g):
            send_xg(0, g, k).wait_recv()
            add_rows(oy, YN, k * tile, tile, rx.at[2, span(k * tile, tile)], g * group, group)
            send_yg(g, k).start()
            return carry

        lax.fori_loop(0, n_tile, pass_two, 0)
        if g == 0:
            close_two(1, OWN)

    def add_first(k, carry):
        at = span(k * tile, tile)
        send_x(1, k).wait_recv()
        add_rows(y, OWN, k * tile, tile, rx.at[1, at])
        send_y(k).wait_recv()
        add_rows(oy, OWN, k * tile, tile, ry.at[0, at])
        return carry

    def add_second(k, carry):
        at = span(k * tile, tile)
        send_yg(0, k).wait_recv()
        add_rows(y, OWN, k * tile, tile, ry.at[1, at], 0, group)
        send_xg(1, 0, k).wait_recv()
        add_rows(oy, OWN, k * tile, tile, rx.at[3, at], 0, group)
        return carry

    lax.fori_loop(0, n_tile, add_first, 0)
    lax.fori_loop(0, n_tile, add_second, 0)

    def result(k):
        return pltpu.make_async_copy(tok.at[span(k * tile, tile)], out_hbm.at[span(k * tile, tile)], out_sem.at[k])

    def last_add(k, carry):
        at = span(k * tile, tile)
        send_yg(1, k).wait_recv()
        add_rows(y, OWN, k * tile, tile, ry.at[1, at], group, group)
        send_xg(1, 1, k).wait_recv()
        add_rows(oy, OWN, k * tile, tile, rx.at[3, at], group, group)
        for part in range(2):
            cols = pl.ds(part * half_w, half_w)
            tok[at, cols] = (tok[at, cols].astype(jnp.float32) + acc[part, at, :]).astype(tok.dtype)
        result(k).start()
        return carry

    lax.fori_loop(0, n_tile, last_add, 0)

    def drain_w(i, carry):
        for m in range(3):
            partner_own(m, i).wait_send()
        for m in range(2):
            send_w(m, i).wait_send()
            partner_fwd(m, i).wait_send()
        for g in range(2):
            send_d(g, i).wait_send()
            fwd_d(g, i).wait_send()
        return carry

    lax.fori_loop(0, n_own, drain_w, 0)
    for k in range(n_first):
        send_x(0, k).wait_send()

    def drain_c(k, carry):
        send_x(1, k).wait_send()
        send_y(k).wait_send()
        for g in range(2):
            send_xg(0, g, k).wait_send()
            send_xg(1, g, k).wait_send()
            send_yg(g, k).wait_send()
        result(k).wait()
        return carry

    lax.fori_loop(0, n_tile, drain_c, 0)
    for cp in (spill, tok_x, tok_y, tok_d, g_x, g_y, g_d):
        cp.wait_send()


def solution(mesh):
    ep_size = mesh.shape["ep"]
    row_spec = P(("rep", "ep", "fsdp"), None)

    def device_step(tokens, expert_idx, gates, w_gate, w_up, w_down):
        rows, top_k = expert_idx.shape
        n_local, half_w, ffn = w_gate.shape
        width = tokens.shape[1]
        n_own = n_local // 2
        num_experts = n_local * ep_size
        capacity = (2 * rows * top_k + num_experts - 1) // num_experts
        chunk, spill_rows = 64, 32
        n_chunk, n_tile = rows // chunk, rows // (2 * chunk)
        dma = pltpu.SemaphoreType.DMA
        hbm = pl.BlockSpec(memory_space=pl.ANY)
        return pl.pallas_call(
            functools.partial(moe_kernel, num_experts, capacity, chunk, spill_rows),
            out_shape=jax.ShapeDtypeStruct((rows, width), jnp.bfloat16),
            in_specs=[hbm] * 6,
            out_specs=hbm,
            scratch_shapes=[
                pltpu.VMEM((top_k, rows), jnp.int32),
                pltpu.VMEM((top_k, rows), jnp.float32),
                pltpu.VMEM((4 * rows, width), jnp.bfloat16),
                pltpu.VMEM((3, n_local, 2, half_w, ffn), jnp.bfloat16),
                pltpu.VMEM((2, 4 * rows, half_w), jnp.float32),
                pltpu.VMEM((n_local, 4 * rows, ffn), jnp.bfloat16),
                pltpu.VMEM((num_experts, rows), jnp.float32),
                pltpu.VMEM((4 * n_local, rows), jnp.float32),
                pltpu.VMEM((4 * rows, 128), jnp.float32),
                pltpu.VMEM((4, rows, half_w), jnp.float32),
                pltpu.VMEM((2, rows, half_w), jnp.float32),
                pltpu.VMEM((spill_rows, half_w), jnp.float32),
                dma((2,)), dma((n_tile,)), dma, dma((3,)), dma((3,)), dma((3,)), dma((3,)),
                dma((3, n_own)), dma((3, n_own)), dma((3, n_own)),
                dma((3, n_own)), dma((3, n_own)), dma((2, n_own)), dma((2, n_own)),
                dma((2, n_own)), dma((2, n_own)), dma((2, n_own)), dma((2, n_own)),
                dma((6, n_tile + 1)), dma((6, n_tile + 1)), dma((3, n_tile)), dma((3, n_tile)), dma, dma,
            ],
            compiler_params=pltpu.CompilerParams(collective_id=0, has_side_effects=True, vmem_limit_bytes=67_043_328),
        )(tokens, expert_idx.T, gates.T, w_gate, w_up, w_down)

    return jax.shard_map(device_step, mesh=mesh, in_specs=(row_spec, row_spec, row_spec, P("ep", "fsdp", None), P("ep", "fsdp", None), P("ep", None, "fsdp")), out_specs=row_spec, check_vma=False)
```

time: 218 us -> 215 us (0.986)
  no operation moved by 1% of the time
where the time goes in v3:
time: 215 us
  Pallas kernels  213 us (99%)
  local copies, waits for them, and re-layouts  2.26 us (1%)
    pallas_call x1, Pallas kernels, device_step(): pl.pallas_call(functools.partial(moe_kernel, num_experts, capacity, chunk...  213 us

profile of v3, /device:TPU:1, one launch (start us, length us, event | category | flops | bytes accessed | tf_op | source)
XLA Modules:
  0.0 215.1 jit_solution(7260577045178078597)
XLA Ops:
  0.0 212.8 %shard_map.64 = bf16[512,1024]{1,0:T(8,128)(2,1)} custom-call(bf16[512,1024]{1,0:T(8,128)(2,1)} %tokens_hbm.1, s32[8,512]{1,0:T(8,128)} %bitcast.2, f32[8,512]{1,0:T(8,128)} %bitcast.3, bf16[8,512,512]{2,1,0:T(8,128)(2,1)} %wg_hbm.1, bf16[8,512,512]{2,1,0:T(8,128)(2,1)} %wu_hbm.1, bf16[8,512,512]{2,1,0:T(8,128)(2,1)} %wd_hbm.1), custom_call_target="tpu_custom_call" | custom-call | tf_op jit(solution)/shard_map/pallas_call | solution.py:413
  212.8 2.3 %copy.8 = bf16[512,1024]{1,0:T(8,128)(2,1)} copy(bf16[512,1024]{1,0:T(8,128)(2,1)} %shard_map.64) | data formatting | bytes 2097152

commit v4 on v3

--- a/solution.py
+++ b/solution.py
@@ -53,9 +53,12 @@
     tok_x = remote(tokens_hbm, block(XN), tok_send.at[1], tok_recv.at[1], x_dev)
     tok_d = remote(block(YN), block(DG), tok_send.at[2], tok_recv.at[2], x_dev)
     tok_l = pltpu.make_async_copy(tokens_hbm, block(OWN), loc_tok_sem)
-    tok_y.start()
     tok_x.start()
     tok_l.start()
+
+    @pl.when(c == 1)
+    def _():
+        tok_y.start()
 
     row = lax.broadcasted_iota(jnp.int32, (num_experts, 1), 0)
     dest, slot = row // n_local, lax.rem(row, n_local)
@@ -80,7 +83,8 @@
     g_x = remote(gt_send.at[pl.ds(XN * n_local, n_local)], gt_recv.at[pl.ds(0, n_local)], g_send.at[0], g_recv_sem.at[0], x_dev)
     g_y = remote(gt_send.at[pl.ds(YN * n_local, 2 * n_local)], gt_recv.at[pl.ds(n_local, 2 * n_local)], g_send.at[1], g_recv_sem.at[1], y_dev)
     g_d = remote(gt_recv.at[pl.ds(2 * n_local, n_local)], gt_recv.at[pl.ds(3 * n_local, n_local)], g_send.at[2], g_recv_sem.at[2], x_dev)
-    g_y.start()
+
+
     g_x.start()
 
     def local_w(m, i):
@@ -110,16 +114,33 @@
     def fwd_d(g, i):
         return remote(down_half(i, oy, g), down_half(n_own + i, oy, g), df_s.at[g, i], df_r.at[g, i], p_dev)
 
-    for i in range(n_own):
-        for m in range(2):
-            send_w(m, i).start()
-    for g in range(2):
+    def send_gate_up():
         for i in range(n_own):
-            send_d(g, i).start()
+            for m in range(2):
+                send_w(m, i).start()
+
+    @pl.when(c == 1)
+    def _():
+        g_y.start()
+        send_gate_up()
+
+    def send_down():
+        for g in range(2):
+            for i in range(n_own):
+                send_d(g, i).start()
+
     for i in range(n_own):
         for m in range(3):
             local_w(m, i).start()
             partner_own(m, i).start()
+
+    @pl.when(c == 0)
+    def _():
+        local_w(0, 0).wait()
+        tok_y.start()
+        g_y.start()
+        send_gate_up()
+        send_down()
 
     def clear(k, carry):
         for part in range(2):
@@ -178,7 +199,12 @@
     def round_one(i, carry):
         for m in range(2):
             arrive(m, i)
-            local_w(m, i).wait()
+
+        @pl.when((i > 0) | (c == 1))
+        def _():
+            local_w(0, i).wait()
+
+        local_w(1, i).wait()
         local_w(2, i).wait()
 
         def both(s):
@@ -202,34 +228,37 @@
 
     last = n_own - 1
     tile = 2 * chunk
-    n_tile = rows // tile
     kept = rows - spill_rows
-    starts = [0, tile // 2, *range(tile, kept, tile)]
+    starts = [0, tile // 2, tile, 2 * tile]
     pieces = [(a, b - a) for a, b in zip(starts, [*starts[1:], kept])]
     n_first = len(pieces)
-
-    def part_of(part, b, start, n):
-        return acc.at[part, span(b * rows + start, n)]
-
-    def send_x(kind, k):
-        start, n = pieces[k] if kind == 0 else (k * tile, tile)
-        return remote(part_of(y, (DG, XN)[kind], start, n), rx.at[kind, span(start, n)], cx_s.at[kind, k], cx_r.at[kind, k], x_dev)
-
-    def send_xg(kind, g, k):
-        cols = pl.ds(g * group, group)
-        sem = 2 + 2 * kind + g
-        return remote(acc.at[oy, span((DG, XN)[kind] * rows + k * tile, tile), cols], rx.at[2 + kind, span(k * tile, tile), cols],
-                      cx_s.at[sem, k], cx_r.at[sem, k], x_dev)
-
-    def send_y(k):
-        return remote(part_of(y, YN, k * tile, tile), ry.at[0, span(k * tile, tile)], cy_s.at[0, k], cy_r.at[0, k], y_dev)
-
-    def send_yg(g, k):
-        cols = pl.ds(g * group, group)
-        return remote(acc.at[oy, span(YN * rows + k * tile, tile), cols], ry.at[1, span(k * tile, tile), cols],
-                      cy_s.at[1 + g, k], cy_r.at[1 + g, k], y_dev)
-
-    spill = remote(part_of(y, DG, kept, spill_rows), ry_spill, spill_s, spill_r, y_dev)
+    whole = [(0, rows)]
+    fine = [(0, rows - tile), (rows - tile, tile - 32), (rows - 32, 32)]
+
+    x_pieces = {(DG, 0): pieces, (XN, 0): whole, (DG, 1): whole, (DG, 2): whole, (XN, 1): whole, (XN, 2): fine}
+    y_pieces = (whole, whole, fine)
+    x_places = {kind: n for n, kind in enumerate(x_pieces)}
+    landing = {DG: 0, XN: 1}
+
+    def sums(stage, b, start, n):
+        at = span(b * rows + start, n)
+        return acc.at[y, at] if stage == 0 else acc.at[oy, at, pl.ds((stage - 1) * group, group)]
+
+    def landed(buffer, slot, stage, start, n):
+        at = span(start, n)
+        return buffer.at[slot, at] if stage == 0 else buffer.at[slot, at, pl.ds((stage - 1) * group, group)]
+
+    def send_x(b, stage, k):
+        start, n = x_pieces[b, stage][k]
+        slot = landing[b] + (2 if stage else 0)
+        sem = x_places[b, stage]
+        return remote(sums(stage, b, start, n), landed(rx, slot, stage, start, n), cx_s.at[sem, k], cx_r.at[sem, k], x_dev)
+
+    def send_y(stage, k):
+        start, n = y_pieces[stage][k]
+        return remote(sums(stage, YN, start, n), landed(ry, 1 if stage else 0, stage, start, n), cy_s.at[stage, k], cy_r.at[stage, k], y_dev)
+
+    spill = remote(sums(0, DG, kept, spill_rows), ry_spill, spill_s, spill_r, y_dev)
 
     def add_rows(part, b, start, n, got, col=0, n_col=half_w):
         at, cols = span(b * rows + start, n), pl.ds(col, n_col)
@@ -240,14 +269,27 @@
         first = acc[part, at, cols] + weighted(last, start, n, part, col, n_col)
         acc[part, at, cols] = first + weighted(n_own + last, start, n, part, col, n_col)
 
-    for m in range(2):
-        arrive(m, last)
+    arrive(0, last)
+    for m in range(3):
         local_w(m, last).wait()
-    local_w(2, last).wait()
-    for m in range(2):
         partner_own(m, last).wait_recv()
-        partner_fwd(m, last).wait_recv()
-    partner_own(2, last).wait_recv()
+    partner_fwd(0, last).wait_recv()
+    head_start, head = DG * rows, pieces[0][1]
+
+    @pl.when(c == 1)
+    def _():
+        arrive(1, last)
+        gate_up(last, head_start, head)
+        partner_fwd(1, last).wait_recv()
+        send_down()
+        gate_up(n_own + last, head_start, head)
+
+    @pl.when(c == 0)
+    def _():
+        partner_fwd(1, last).wait_recv()
+        gate_up(n_own + last, head_start, head)
+        arrive(1, last)
+        gate_up(last, head_start, head)
 
     def close_one(b, start, n):
         start = b * rows + start
@@ -255,17 +297,15 @@
         gate_up(n_own + last, start, n)
         finish(y, start, n)
 
-    def x_one(k, carry):
-        close_one(XN, k * tile, tile)
-        send_x(1, k).start()
-        return carry
-
-    for k, (start, n) in enumerate(pieces):
+    finish(y, head_start, head)
+    send_x(DG, 0, 0).start()
+    for k, (start, n) in enumerate(pieces[1:], 1):
         close_one(DG, start, n)
-        send_x(0, k).start()
+        send_x(DG, 0, k).start()
     close_one(DG, kept, spill_rows)
     spill.start()
-    lax.fori_loop(0, n_tile, x_one, 0)
+    close_one(XN, 0, rows)
+    send_x(XN, 0, 0).start()
     close_one(YN, 0, rows)
     close_one(OWN, 0, rows)
 
@@ -287,83 +327,67 @@
     arrive_d(0, last)
     fwd_d(0, last).wait_recv()
 
-    def diag_two(k, carry, g=0):
-        finish(oy, DG * rows + k * tile, tile, g * group, group)
-        send_xg(0, g, k).start()
+    def add_x(part, b, stage, k):
+        start, n = x_pieces[b, stage][k]
+        send_x(b, stage, k).wait_recv()
+        slot = landing[b] + (2 if stage else 0)
+        add_rows(part, YN if b == DG else OWN, start, n, rx.at[slot, span(start, n)], *columns(stage))
+
+    def add_y(part, stage, k):
+        start, n = y_pieces[stage][k]
+        send_y(stage, k).wait_recv()
+        add_rows(part, OWN, start, n, ry.at[1 if stage else 0, span(start, n)], *columns(stage))
+
+    def columns(stage):
+        return (0, half_w) if stage == 0 else ((stage - 1) * group, group)
+
+    close_two(0, DG)
+    send_x(DG, 1, 0).start()
+
+    def others(b, carry):
+        close_two(0, b)
         return carry
 
-    lax.fori_loop(0, n_tile, functools.partial(diag_two, g=0), 0)
-    for b in (XN, YN, OWN):
-        close_two(0, b)
-
-    for k, (start, n) in enumerate(pieces):
-        send_x(0, k).wait_recv()
-        add_rows(y, YN, start, n, rx.at[0, span(start, n)])
-        if k > 0:
-            send_y(k - 1).start()
+    lax.fori_loop(OWN, DG, others, 0)
+    for k in range(n_first):
+        add_x(y, DG, 0, k)
+    send_y(0, 0).start()
 
     lax.fori_loop(0, n_own - 1, functools.partial(round_two, g=1), 0)
     arrive_d(1, last)
     fwd_d(1, last).wait_recv()
-    lax.fori_loop(0, n_tile, functools.partial(diag_two, g=1), 0)
+    close_two(1, DG)
+    send_x(DG, 2, 0).start()
     spill.wait_recv()
     add_rows(oy, XN, kept, spill_rows, ry_spill)
-    for k in range(n_tile):
-        send_xg(1, 0, k).start()
-
-    def x_two(k, carry):
-        finish(oy, XN * rows + k * tile, tile, group, group)
-        send_xg(1, 1, k).start()
-        return carry
-
-    lax.fori_loop(0, n_tile, x_two, 0)
+    send_x(XN, 1, 0).start()
+    close_two(1, XN)
+    for k in range(len(fine)):
+        send_x(XN, 2, k).start()
     close_two(1, YN)
-    for g in range(2):
-        def pass_two(k, carry, g=g):
-            send_xg(0, g, k).wait_recv()
-            add_rows(oy, YN, k * tile, tile, rx.at[2, span(k * tile, tile)], g * group, group)
-            send_yg(g, k).start()
-            return carry
-
-        lax.fori_loop(0, n_tile, pass_two, 0)
-        if g == 0:
-            close_two(1, OWN)
-
-    def add_first(k, carry):
-        at = span(k * tile, tile)
-        send_x(1, k).wait_recv()
-        add_rows(y, OWN, k * tile, tile, rx.at[1, at])
-        send_y(k).wait_recv()
-        add_rows(oy, OWN, k * tile, tile, ry.at[0, at])
-        return carry
-
-    def add_second(k, carry):
-        at = span(k * tile, tile)
-        send_yg(0, k).wait_recv()
-        add_rows(y, OWN, k * tile, tile, ry.at[1, at], 0, group)
-        send_xg(1, 0, k).wait_recv()
-        add_rows(oy, OWN, k * tile, tile, rx.at[3, at], 0, group)
-        return carry
-
-    lax.fori_loop(0, n_tile, add_first, 0)
-    lax.fori_loop(0, n_tile, add_second, 0)
+    add_x(oy, DG, 1, 0)
+    send_y(1, 0).start()
+    close_two(1, OWN)
+    add_x(oy, DG, 2, 0)
+    for k in range(len(fine)):
+        send_y(2, k).start()
+    add_x(y, XN, 0, 0)
+    add_y(oy, 0, 0)
+    add_y(y, 1, 0)
+    add_x(oy, XN, 1, 0)
 
     def result(k):
-        return pltpu.make_async_copy(tok.at[span(k * tile, tile)], out_hbm.at[span(k * tile, tile)], out_sem.at[k])
-
-    def last_add(k, carry):
-        at = span(k * tile, tile)
-        send_yg(1, k).wait_recv()
-        add_rows(y, OWN, k * tile, tile, ry.at[1, at], group, group)
-        send_xg(1, 1, k).wait_recv()
-        add_rows(oy, OWN, k * tile, tile, rx.at[3, at], group, group)
+        start, n = fine[k]
+        return pltpu.make_async_copy(tok.at[span(start, n)], out_hbm.at[span(start, n)], out_sem.at[k])
+
+    for k, (start, n) in enumerate(fine):
+        at = span(start, n)
+        add_y(y, 2, k)
+        add_x(oy, XN, 2, k)
         for part in range(2):
             cols = pl.ds(part * half_w, half_w)
             tok[at, cols] = (tok[at, cols].astype(jnp.float32) + acc[part, at, :]).astype(tok.dtype)
         result(k).start()
-        return carry
-
-    lax.fori_loop(0, n_tile, last_add, 0)
 
     def drain_w(i, carry):
         for m in range(3):
@@ -377,22 +401,16 @@
         return carry
 
     lax.fori_loop(0, n_own, drain_w, 0)
-    for k in range(n_first):
-        send_x(0, k).wait_send()
-
-    def drain_c(k, carry):
-        send_x(1, k).wait_send()
-        send_y(k).wait_send()
-        for g in range(2):
-            send_xg(0, g, k).wait_send()
-            send_xg(1, g, k).wait_send()
-            send_yg(g, k).wait_send()
-        result(k).wait()
-        return carry
-
-    lax.fori_loop(0, n_tile, drain_c, 0)
+    for (b, stage), some in x_pieces.items():
+        for k in range(len(some)):
+            send_x(b, stage, k).wait_send()
+    for stage, some in enumerate(y_pieces):
+        for k in range(len(some)):
+            send_y(stage, k).wait_send()
     for cp in (spill, tok_x, tok_y, tok_d, g_x, g_y, g_d):
         cp.wait_send()
+    for k in range(len(fine)):
+        result(k).wait()
 
 
 def solution(mesh):
@@ -407,7 +425,6 @@
         num_experts = n_local * ep_size
         capacity = (2 * rows * top_k + num_experts - 1) // num_experts
         chunk, spill_rows = 64, 32
-        n_chunk, n_tile = rows // chunk, rows // (2 * chunk)
         dma = pltpu.SemaphoreType.DMA
         hbm = pl.BlockSpec(memory_space=pl.ANY)
         return pl.pallas_call(
@@ -428,11 +445,11 @@
                 pltpu.VMEM((4, rows, half_w), jnp.float32),
                 pltpu.VMEM((2, rows, half_w), jnp.float32),
                 pltpu.VMEM((spill_rows, half_w), jnp.float32),
-                dma((2,)), dma((n_tile,)), dma, dma((3,)), dma((3,)), dma((3,)), dma((3,)),
+                dma((2,)), dma((3,)), dma, dma((3,)), dma((3,)), dma((3,)), dma((3,)),
                 dma((3, n_own)), dma((3, n_own)), dma((3, n_own)),
                 dma((3, n_own)), dma((3, n_own)), dma((2, n_own)), dma((2, n_own)),
                 dma((2, n_own)), dma((2, n_own)), dma((2, n_own)), dma((2, n_own)),
-                dma((6, n_tile + 1)), dma((6, n_tile + 1)), dma((3, n_tile)), dma((3, n_tile)), dma, dma,
+                dma((6, 4)), dma((6, 4)), dma((3, 3)), dma((3, 3)), dma, dma,
             ],
             compiler_params=pltpu.CompilerParams(collective_id=0, has_side_effects=True, vmem_limit_bytes=67_043_328),
         )(tokens, expert_idx.T, gates.T, w_gate, w_up, w_down)

time: 215 us -> 214 us (level)
  no operation moved by 1% of the time
where the time goes in v4:
time: 214 us
  Pallas kernels  212 us (99%)
  local copies, waits for them, and re-layouts  2.26 us (1%)
    pallas_call x1, Pallas kernels, device_step(): pl.pallas_call(functools.partial(moe_kernel, num_experts, capacity, chunk...  212 us

profile of v4, /device:TPU:1, one launch (start us, length us, event | category | flops | bytes accessed | tf_op | source)
XLA Modules:
  0.0 213.9 jit_solution(1861476595378913803)
XLA Ops:
  0.0 211.6 %shard_map.64 = bf16[512,1024]{1,0:T(8,128)(2,1)} custom-call(bf16[512,1024]{1,0:T(8,128)(2,1)} %tokens_hbm.1, s32[8,512]{1,0:T(8,128)} %bitcast.2, f32[8,512]{1,0:T(8,128)} %bitcast.3, bf16[8,512,512]{2,1,0:T(8,128)(2,1)} %wg_hbm.1, bf16[8,512,512]{2,1,0:T(8,128)(2,1)} %wu_hbm.1, bf16[8,512,512]{2,1,0:T(8,128)(2,1)} %wd_hbm.1), custom_call_target="tpu_custom_call" | custom-call | tf_op jit(solution)/shard_map/pallas_call | solution.py:430
  211.6 2.3 %copy.8 = bf16[512,1024]{1,0:T(8,128)(2,1)} copy(bf16[512,1024]{1,0:T(8,128)(2,1)} %shard_map.64) | data formatting | bytes 2097152

commit v5 on v4

--- a/solution.py
+++ b/solution.py
@@ -11,10 +11,10 @@
 OWN, XN, YN, DG = 0, 1, 2, 3
 
 
-def moe_kernel(num_experts, capacity, chunk, spill_rows, tokens_hbm, idx_hbm, gates_hbm, wg_hbm, wu_hbm, wd_hbm, out_hbm,
-               idx_ref, gates_ref, tok, w, acc, hid, gt_send, gt_recv, gcol, rx, ry, ry_spill,
+def moe_kernel(num_experts, capacity, chunk, late_rows, tokens_hbm, idx_hbm, gates_hbm, wg_hbm, wu_hbm, wd_hbm, out_hbm,
+               idx_ref, gates_ref, tok, w, acc, hid, gt_send, gt_recv, gcol, gcol_x, rx, ry, o_out, o_in, go_sem,
                small_sem, out_sem, loc_tok_sem, tok_send, tok_recv, g_send, g_recv_sem, loc_sem, ys_sem, yr_sem,
-               po_s, po_r, pf_s, pf_r, ds_sem, dr_sem, df_s, df_r, cx_s, cx_r, cy_s, cy_r, spill_s, spill_r):
+               po_s, po_r, pf_s, pf_r, ds_sem, dr_sem, df_s, df_r, cx_s, cx_r, cy_s, cy_r, o_s, o_r):
     rows, width = out_hbm.shape
     n_local = wg_hbm.shape[0]
     n_own = n_local // 2
@@ -134,25 +134,34 @@
             local_w(m, i).start()
             partner_own(m, i).start()
 
+    def clear(k, carry):
+        for part in range(2):
+            acc[part, span(k * chunk, chunk), :] = jnp.zeros((chunk, half_w), jnp.float32)
+        return carry
+
+    lax.fori_loop(0, 4 * n_chunk, clear, 0)
+
+    @pl.when(c == 1)
+    def _():
+        tok_y.wait_send()
+        pl.semaphore_signal(go_sem, inc=1, device_id=p_dev, device_id_type=MESH)
+
     @pl.when(c == 0)
     def _():
-        local_w(0, 0).wait()
+        pl.semaphore_wait(go_sem, 1)
         tok_y.start()
         g_y.start()
         send_gate_up()
         send_down()
 
-    def clear(k, carry):
-        for part in range(2):
-            acc[part, span(k * chunk, chunk), :] = jnp.zeros((chunk, half_w), jnp.float32)
-        return carry
-
-    lax.fori_loop(0, 4 * n_chunk, clear, 0)
+    def columns_of(g):
+        return jnp.concatenate([g, jnp.zeros((128 - n_local, rows), jnp.float32)], axis=0).T
 
     def column_gates(b, g):
-        gcol[pl.ds(b * rows, rows), :] = jnp.concatenate([g, jnp.zeros((128 - n_local, rows), jnp.float32)], axis=0).T
+        gcol[pl.ds(b * rows, rows), :] = columns_of(g)
 
     column_gates(OWN, gt_send[0:n_local, :])
+    gcol_x[...] = columns_of(gt_send[pl.ds(XN * n_local, n_local), :])
     tok_y.wait_recv()
     tok_d.start()
     g_y.wait_recv()
@@ -176,11 +185,15 @@
         u = jnp.dot(r, w[1, s].reshape(width, w.shape[-1]), preferred_element_type=jnp.float32)
         hid[s, at, :] = (a * jax.nn.sigmoid(a) * u).astype(jnp.bfloat16)
 
+    def expert_rows(s, start, n, part, col=0, n_col=half_w):
+        return jnp.dot(hid[s, span(start, n), :], w[2, s, part, :, pl.ds(col, n_col)], preferred_element_type=jnp.float32).astype(jnp.bfloat16)
+
+    def scaled(gates, s, o):
+        g = jnp.sum(jnp.where(lane == s, gates, 0.0), axis=1, keepdims=True)
+        return jnp.where(g != 0.0, g * o.astype(jnp.float32), 0.0)
+
     def weighted(s, start, n, part, col=0, n_col=half_w):
-        at = span(start, n)
-        g = jnp.sum(jnp.where(lane == s, gcol[at, :], 0.0), axis=1, keepdims=True)
-        o = jnp.dot(hid[s, at, :], w[2, s, part, :, pl.ds(col, n_col)], preferred_element_type=jnp.float32).astype(jnp.bfloat16).astype(jnp.float32)
-        return jnp.where(g != 0.0, g * o, 0.0)
+        return scaled(gcol[span(start, n), :], s, expert_rows(s, start, n, part, col, n_col))
 
     def down(s, g):
         cols = pl.ds(g * group, group)
@@ -196,46 +209,58 @@
         arrived_w(m, i).wait_recv()
         partner_fwd(m, i).start()
 
-    def round_one(i, carry):
+    def await_own(i):
         for m in range(2):
             arrive(m, i)
-
-        @pl.when((i > 0) | (c == 1))
-        def _():
-            local_w(0, i).wait()
-
-        local_w(1, i).wait()
-        local_w(2, i).wait()
-
-        def both(s):
-            def step(b, carry):
-                at = span(b * rows, rows)
-                gate_up(s, b * rows, rows)
-                acc[y, at, :] = acc[y, at, :] + weighted(s, b * rows, rows, y)
-                return carry
-
-            lax.fori_loop(0, 4, step, 0)
-
-        both(i)
+        for m in range(3):
+            local_w(m, i).wait()
+
+    def await_partner(i):
+        for m in range(3):
+            partner_own(m, i).wait_recv()
         for m in range(2):
-            partner_own(m, i).wait_recv()
             partner_fwd(m, i).wait_recv()
-        partner_own(2, i).wait_recv()
-        both(n_own + i)
+
+    def await_first(i):
+        pl.when(c == 0)(functools.partial(await_partner, i))
+        pl.when(c == 1)(functools.partial(await_own, i))
+        return i + n_own * (1 - c)
+
+    def await_second(i):
+        pl.when(c == 0)(functools.partial(await_own, i))
+        pl.when(c == 1)(functools.partial(await_partner, i))
+        return i + n_own * c
+
+    def apply(s, b, start, n):
+        start = b * rows + start
+        at = span(start, n)
+        gate_up(s, start, n)
+        acc[y, at, :] = acc[y, at, :] + weighted(s, start, n, y)
+
+    def all_rows(s):
+        def step(b, carry):
+            apply(s, b, 0, rows)
+            return carry
+
+        lax.fori_loop(0, 4, step, 0)
+
+    def round_one(i, carry):
+        all_rows(await_first(i))
+        all_rows(await_second(i))
         return carry
 
-    lax.fori_loop(0, n_own - 1, round_one, 0)
-
     last = n_own - 1
+    lax.fori_loop(0, last - 1, round_one, 0)
+    all_rows(await_first(last - 1))
+
     tile = 2 * chunk
-    kept = rows - spill_rows
-    starts = [0, tile // 2, tile, 2 * tile]
-    pieces = [(a, b - a) for a, b in zip(starts, [*starts[1:], kept])]
+    kept = rows - late_rows
+    pieces = [(0, chunk), (chunk, chunk), (tile, tile), (2 * tile, rows - 2 * tile)]
     n_first = len(pieces)
     whole = [(0, rows)]
     fine = [(0, rows - tile), (rows - tile, tile - 32), (rows - 32, 32)]
 
-    x_pieces = {(DG, 0): pieces, (XN, 0): whole, (DG, 1): whole, (DG, 2): whole, (XN, 1): whole, (XN, 2): fine}
+    x_pieces = {(DG, 0): pieces, (XN, 0): [(kept, late_rows), (0, kept)], (DG, 1): whole, (DG, 2): whole, (XN, 1): whole, (XN, 2): fine}
     y_pieces = (whole, whole, fine)
     x_places = {kind: n for n, kind in enumerate(x_pieces)}
     landing = {DG: 0, XN: 1}
@@ -258,7 +283,7 @@
         start, n = y_pieces[stage][k]
         return remote(sums(stage, YN, start, n), landed(ry, 1 if stage else 0, stage, start, n), cy_s.at[stage, k], cy_r.at[stage, k], y_dev)
 
-    spill = remote(sums(0, DG, kept, spill_rows), ry_spill, spill_s, spill_r, y_dev)
+    late_o = remote(o_out, o_in, o_s, o_r, x_dev)
 
     def add_rows(part, b, start, n, got, col=0, n_col=half_w):
         at, cols = span(b * rows + start, n), pl.ds(col, n_col)
@@ -269,45 +294,26 @@
         first = acc[part, at, cols] + weighted(last, start, n, part, col, n_col)
         acc[part, at, cols] = first + weighted(n_own + last, start, n, part, col, n_col)
 
-    arrive(0, last)
-    for m in range(3):
-        local_w(m, last).wait()
-        partner_own(m, last).wait_recv()
-    partner_fwd(0, last).wait_recv()
-    head_start, head = DG * rows, pieces[0][1]
-
-    @pl.when(c == 1)
-    def _():
-        arrive(1, last)
-        gate_up(last, head_start, head)
-        partner_fwd(1, last).wait_recv()
-        send_down()
-        gate_up(n_own + last, head_start, head)
-
-    @pl.when(c == 0)
-    def _():
-        partner_fwd(1, last).wait_recv()
-        gate_up(n_own + last, head_start, head)
-        arrive(1, last)
-        gate_up(last, head_start, head)
-
-    def close_one(b, start, n):
-        start = b * rows + start
-        gate_up(last, start, n)
-        gate_up(n_own + last, start, n)
-        finish(y, start, n)
-
-    finish(y, head_start, head)
-    send_x(DG, 0, 0).start()
-    for k, (start, n) in enumerate(pieces[1:], 1):
-        close_one(DG, start, n)
+    before_last = await_second(last - 1)
+    apply(before_last, XN, 0, rows)
+    early = await_first(last)
+    apply(early, XN, 0, rows)
+    send_x(XN, 0, 0).start()
+    apply(before_last, DG, 0, rows)
+    apply(early, DG, 0, rows)
+    late = await_second(last)
+    pl.when(c == 1)(send_down)
+    for k, (start, n) in enumerate(pieces):
+        apply(late, DG, start, n)
         send_x(DG, 0, k).start()
-    close_one(DG, kept, spill_rows)
-    spill.start()
-    close_one(XN, 0, rows)
-    send_x(XN, 0, 0).start()
-    close_one(YN, 0, rows)
-    close_one(OWN, 0, rows)
+    gate_up(late, XN * rows + kept, late_rows)
+    o_out[...] = expert_rows(late, XN * rows + kept, late_rows, y)
+    late_o.start()
+    apply(late, XN, 0, kept)
+    send_x(XN, 0, 1).start()
+    for s in (before_last, early, late):
+        for b in (YN, OWN):
+            apply(s, b, 0, rows)
 
     def arrive_d(g, i):
         arrived_d(g, i).wait_recv()
@@ -358,8 +364,6 @@
     fwd_d(1, last).wait_recv()
     close_two(1, DG)
     send_x(DG, 2, 0).start()
-    spill.wait_recv()
-    add_rows(oy, XN, kept, spill_rows, ry_spill)
     send_x(XN, 1, 0).start()
     close_two(1, XN)
     for k in range(len(fine)):
@@ -372,6 +376,10 @@
     for k in range(len(fine)):
         send_y(2, k).start()
     add_x(y, XN, 0, 0)
+    add_x(y, XN, 0, 1)
+    late_o.wait_recv()
+    at_late = span(kept, late_rows)
+    acc[y, at_late, :] = acc[y, at_late, :] + scaled(gcol_x[at_late, :], late, o_in[...])
     add_y(oy, 0, 0)
     add_y(y, 1, 0)
     add_x(oy, XN, 1, 0)
@@ -407,7 +415,8 @@
     for stage, some in enumerate(y_pieces):
         for k in range(len(some)):
             send_y(stage, k).wait_send()
-    for cp in (spill, tok_x, tok_y, tok_d, g_x, g_y, g_d):
+    pl.when(c == 0)(tok_y.wait_send)
+    for cp in (late_o, tok_x, tok_d, g_x, g_y, g_d):
         cp.wait_send()
     for k in range(len(fine)):
         result(k).wait()
@@ -424,11 +433,11 @@
         n_own = n_local // 2
         num_experts = n_local * ep_size
         capacity = (2 * rows * top_k + num_experts - 1) // num_experts
-        chunk, spill_rows = 64, 32
+        chunk, late_rows = 64, 128
         dma = pltpu.SemaphoreType.DMA
         hbm = pl.BlockSpec(memory_space=pl.ANY)
         return pl.pallas_call(
-            functools.partial(moe_kernel, num_experts, capacity, chunk, spill_rows),
+            functools.partial(moe_kernel, num_experts, capacity, chunk, late_rows),
             out_shape=jax.ShapeDtypeStruct((rows, width), jnp.bfloat16),
             in_specs=[hbm] * 6,
             out_specs=hbm,
@@ -442,9 +451,12 @@
                 pltpu.VMEM((num_experts, rows), jnp.float32),
                 pltpu.VMEM((4 * n_local, rows), jnp.float32),
                 pltpu.VMEM((4 * rows, 128), jnp.float32),
+                pltpu.VMEM((rows, 128), jnp.float32),
                 pltpu.VMEM((4, rows, half_w), jnp.float32),
                 pltpu.VMEM((2, rows, half_w), jnp.float32),
-                pltpu.VMEM((spill_rows, half_w), jnp.float32),
+                pltpu.VMEM((late_rows, half_w), jnp.bfloat16),
+                pltpu.VMEM((late_rows, half_w), jnp.bfloat16),
+                pltpu.SemaphoreType.REGULAR,
                 dma((2,)), dma((3,)), dma, dma((3,)), dma((3,)), dma((3,)), dma((3,)),
                 dma((3, n_own)), dma((3, n_own)), dma((3, n_own)),
                 dma((3, n_own)), dma((3, n_own)), dma((2, n_own)), dma((2, n_own)),

time: 214 us -> 212 us (level)
  no operation moved by 1% of the time
where the time goes in v5:
time: 212 us
  Pallas kernels  210 us (99%)
  local copies, waits for them, and re-layouts  2.26 us (1%)
    pallas_call x1, Pallas kernels, device_step(): pl.pallas_call(functools.partial(moe_kernel, num_experts, capacity, chunk...  210 us

profile of v5, /device:TPU:1, one launch (start us, length us, event | category | flops | bytes accessed | tf_op | source)
XLA Modules:
  0.0 212.2 jit_solution(556970964599742448)
XLA Ops:
  0.0 209.9 %shard_map.64 = bf16[512,1024]{1,0:T(8,128)(2,1)} custom-call(bf16[512,1024]{1,0:T(8,128)(2,1)} %tokens_hbm.1, s32[8,512]{1,0:T(8,128)} %bitcast.2, f32[8,512]{1,0:T(8,128)} %bitcast.3, bf16[8,512,512]{2,1,0:T(8,128)(2,1)} %wg_hbm.1, bf16[8,512,512]{2,1,0:T(8,128)(2,1)} %wu_hbm.1, bf16[8,512,512]{2,1,0:T(8,128)(2,1)} %wd_hbm.1), custom_call_target="tpu_custom_call" | custom-call | tf_op jit(solution)/shard_map/pallas_call | solution.py:439
  209.9 2.3 %copy.8 = bf16[512,1024]{1,0:T(8,128)(2,1)} copy(bf16[512,1024]{1,0:T(8,128)(2,1)} %shard_map.64) | data formatting | bytes 2097152

commit v6 on v5

--- a/solution.py
+++ b/solution.py
@@ -197,13 +197,14 @@
 
     def down(s, g):
         cols = pl.ds(g * group, group)
-
-        def step(b, carry):
-            at = span(b * rows, rows)
-            acc[oy, at, cols] = acc[oy, at, cols] + weighted(s, b * rows, rows, oy, g * group, group)
+        step_rows = rows // 2
+
+        def step(k, carry):
+            at = span(k * step_rows, step_rows)
+            acc[oy, at, cols] = acc[oy, at, cols] + weighted(s, k * step_rows, step_rows, oy, g * group, group)
             return carry
 
-        lax.fori_loop(0, 4, step, 0)
+        lax.fori_loop(0, 8, step, 0)
 
     def arrive(m, i):
         arrived_w(m, i).wait_recv()
@@ -232,10 +233,16 @@
         return i + n_own * c
 
     def apply(s, b, start, n):
-        start = b * rows + start
-        at = span(start, n)
-        gate_up(s, start, n)
-        acc[y, at, :] = acc[y, at, :] + weighted(s, start, n, y)
+        size = min(n, rows // 2) if n % (rows // 2) == 0 else n if n < rows // 2 else 2 * chunk
+
+        def step(k, carry):
+            first = b * rows + start + k * size
+            at = span(first, size)
+            gate_up(s, first, size)
+            acc[y, at, :] = acc[y, at, :] + weighted(s, first, size, y)
+            return carry
+
+        lax.fori_loop(0, n // size, step, 0)
 
     def all_rows(s):
         def step(b, carry):
@@ -327,7 +334,11 @@
         return carry
 
     def close_two(g, b):
-        finish(oy, b * rows, rows, g * group, group)
+        def step(k, carry):
+            finish(oy, b * rows + k * (rows // 2), rows // 2, g * group, group)
+            return carry
+
+        lax.fori_loop(0, 2, step, 0)
 
     lax.fori_loop(0, n_own - 1, functools.partial(round_two, g=0), 0)
     arrive_d(0, last)
@@ -392,9 +403,12 @@
         at = span(start, n)
         add_y(y, 2, k)
         add_x(oy, XN, 2, k)
-        for part in range(2):
-            cols = pl.ds(part * half_w, half_w)
-            tok[at, cols] = (tok[at, cols].astype(jnp.float32) + acc[part, at, :]).astype(tok.dtype)
+        cut = n // 2 if n > tile else n
+        for a in range(start, start + n, cut):
+            rows_at = span(a, cut)
+            for part in range(2):
+                cols = pl.ds(part * half_w, half_w)
+                tok[rows_at, cols] = (tok[rows_at, cols].astype(jnp.float32) + acc[part, rows_at, :]).astype(tok.dtype)
         result(k).start()
 
     def drain_w(i, carry):
@@ -438,7 +452,7 @@
         hbm = pl.BlockSpec(memory_space=pl.ANY)
         return pl.pallas_call(
             functools.partial(moe_kernel, num_experts, capacity, chunk, late_rows),
-            out_shape=jax.ShapeDtypeStruct((rows, width), jnp.bfloat16),
+            out_shape=pltpu.VMEM((rows, width), jnp.bfloat16),
             in_specs=[hbm] * 6,
             out_specs=hbm,
             scratch_shapes=[
@@ -463,7 +477,7 @@
                 dma((2, n_own)), dma((2, n_own)), dma((2, n_own)), dma((2, n_own)),
                 dma((6, 4)), dma((6, 4)), dma((3, 3)), dma((3, 3)), dma, dma,
             ],
-            compiler_params=pltpu.CompilerParams(collective_id=0, has_side_effects=True, vmem_limit_bytes=67_043_328),
+            compiler_params=pltpu.CompilerParams(collective_id=0, has_side_effects=True, vmem_limit_bytes=64_900_000),
         )(tokens, expert_idx.T, gates.T, w_gate, w_up, w_down)
 
     return jax.shard_map(device_step, mesh=mesh, in_specs=(row_spec, row_spec, row_spec, P("ep", "fsdp", None), P("ep", "fsdp", None), P("ep", None, "fsdp")), out_specs=row_spec, check_vma=False)

time: 212 us -> 211 us (level)
  no operation moved by 1% of the time
where the time goes in v6:
time: 211 us
  Pallas kernels  210 us (100%)
    pallas_call x1, Pallas kernels, device_step(): pl.pallas_call(functools.partial(moe_kernel, num_experts, capacity, chunk...  210 us

profile of v6, /device:TPU:1, one launch (start us, length us, event | category | flops | bytes accessed | tf_op | source)
XLA Modules:
  0.0 210.8 jit_solution(321238348375832740)
XLA Ops:
  0.0 209.9 %shard_map.64 = bf16[512,1024]{1,0:T(8,128)(2,1)S(1)} custom-call(bf16[512,1024]{1,0:T(8,128)(2,1)} %tokens_hbm.1, s32[8,512]{1,0:T(8,128)} %bitcast.2, f32[8,512]{1,0:T(8,128)} %bitcast.3, bf16[8,512,512]{2,1,0:T(8,128)(2,1)} %wg_hbm.1, bf16[8,512,512]{2,1,0:T(8,128)(2,1)} %wu_hbm.1, bf16[8,512,512]{2,1,0:T(8,128)(2,1)} %wd_hbm.1), custom_call_target="tpu_custom_call" | custom-call | tf_op jit(solution)/shard_map/pallas_call | solution.py:453
  209.9 1.0 copy.8

commit v7 on v6

--- a/solution.py
+++ b/solution.py
@@ -233,7 +233,7 @@
         return i + n_own * c
 
     def apply(s, b, start, n):
-        size = min(n, rows // 2) if n % (rows // 2) == 0 else n if n < rows // 2 else 2 * chunk
+        size = n if n < rows // 2 else rows // 2 if n % (rows // 2) == 0 else n // 2
 
         def step(k, carry):
             first = b * rows + start + k * size
@@ -447,7 +447,7 @@
         n_own = n_local // 2
         num_experts = n_local * ep_size
         capacity = (2 * rows * top_k + num_experts - 1) // num_experts
-        chunk, late_rows = 64, 128
+        chunk, late_rows = 64, 160
         dma = pltpu.SemaphoreType.DMA
         hbm = pl.BlockSpec(memory_space=pl.ANY)
         return pl.pallas_call(

time: 211 us -> 210 us (level)
  no operation moved by 1% of the time
where the time goes in v7:
time: 210 us
  Pallas kernels  209 us (100%)
    pallas_call x1, Pallas kernels, device_step(): pl.pallas_call(functools.partial(moe_kernel, num_experts, capacity, chunk...  209 us

profile of v7, /device:TPU:1, one launch (start us, length us, event | category | flops | bytes accessed | tf_op | source)
XLA Modules:
  0.0 210.2 jit_solution(16212402508164361685)
XLA Ops:
  0.0 209.2 %shard_map.64 = bf16[512,1024]{1,0:T(8,128)(2,1)S(1)} custom-call(bf16[512,1024]{1,0:T(8,128)(2,1)} %tokens_hbm.1, s32[8,512]{1,0:T(8,128)} %bitcast.2, f32[8,512]{1,0:T(8,128)} %bitcast.3, bf16[8,512,512]{2,1,0:T(8,128)(2,1)} %wg_hbm.1, bf16[8,512,512]{2,1,0:T(8,128)(2,1)} %wu_hbm.1, bf16[8,512,512]{2,1,0:T(8,128)(2,1)} %wd_hbm.1), custom_call_target="tpu_custom_call" | custom-call | tf_op jit(solution)/shard_map/pallas_call | solution.py:453
  209.2 1.0 copy.8

commit v8 on v7

--- a/solution.py
+++ b/solution.py
@@ -124,10 +124,14 @@
         g_y.start()
         send_gate_up()
 
+    def all_first(part):
+        return remote(wd_hbm.at[pl.ds(oy * n_own, n_own), :, pl.ds(0, group)], w.at[2, pl.ds(0, n_own), part, :, pl.ds(0, group)],
+                      ds_sem.at[0, 0], dr_sem.at[0, 0], y_dev)
+
     def send_down():
-        for g in range(2):
-            for i in range(n_own):
-                send_d(g, i).start()
+        all_first(y).start()
+        for i in range(n_own):
+            send_d(1, i).start()
 
     for i in range(n_own):
         for m in range(3):
@@ -323,8 +327,9 @@
             apply(s, b, 0, rows)
 
     def arrive_d(g, i):
-        arrived_d(g, i).wait_recv()
-        fwd_d(g, i).start()
+        if g == 1:
+            arrived_d(g, i).wait_recv()
+            fwd_d(g, i).start()
 
     def round_two(i, carry, g=0):
         arrive_d(g, i)
@@ -340,6 +345,9 @@
 
         lax.fori_loop(0, 2, step, 0)
 
+    all_first(oy).wait_recv()
+    for i in range(n_own):
+        fwd_d(0, i).start()
     lax.fori_loop(0, n_own - 1, functools.partial(round_two, g=0), 0)
     arrive_d(0, last)
     fwd_d(0, last).wait_recv()
@@ -417,12 +425,13 @@
         for m in range(2):
             send_w(m, i).wait_send()
             partner_fwd(m, i).wait_send()
+        send_d(1, i).wait_send()
         for g in range(2):
-            send_d(g, i).wait_send()
             fwd_d(g, i).wait_send()
         return carry
 
     lax.fori_loop(0, n_own, drain_w, 0)
+    all_first(y).wait_send()
     for (b, stage), some in x_pieces.items():
         for k in range(len(some)):
             send_x(b, stage, k).wait_send()

time: 210 us -> 212 us (level)
  no operation moved by 1% of the time
where the time goes in v8:
time: 212 us; the launch traced here: 210 us
  Pallas kernels  209 us (99%)
    pallas_call x1, Pallas kernels, device_step(): pl.pallas_call(functools.partial(moe_kernel, num_experts, capacity, chunk...  209 us

profile of v8, /device:TPU:1, one launch (start us, length us, event | category | flops | bytes accessed | tf_op | source)
XLA Modules:
  0.0 210.4 jit_solution(16510184291307029237)
XLA Ops:
  0.0 209.5 %shard_map.64 = bf16[512,1024]{1,0:T(8,128)(2,1)S(1)} custom-call(bf16[512,1024]{1,0:T(8,128)(2,1)} %tokens_hbm.1, s32[8,512]{1,0:T(8,128)} %bitcast.2, f32[8,512]{1,0:T(8,128)} %bitcast.3, bf16[8,512,512]{2,1,0:T(8,128)(2,1)} %wg_hbm.1, bf16[8,512,512]{2,1,0:T(8,128)(2,1)} %wu_hbm.1, bf16[8,512,512]{2,1,0:T(8,128)(2,1)} %wd_hbm.1), custom_call_target="tpu_custom_call" | custom-call | tf_op jit(solution)/shard_map/pallas_call | solution.py:462
  209.5 1.0 copy.8
